TPU v7x, 32 devices: a whole 2x2x4 slice. The times are simulated.
32 devices in a mesh: grp: 2 (over y), row: 4 (over z), col: 2 (over x), slc: 2 (over core).
Axes of the slice: x: 2, y: 2, z: 4, core: 2. Of those that a mesh axis runs over, the one named last changes fastest.
Arguments:
- objects: bfloat16 [2, 2, 3072, 768], P(None, None, ('grp', 'row'), 'col'), parts along dimension 2, may hold values from -1 to 1
- probes: bfloat16 [4, 2, 256, 256], P(('grp', 'slc')), parts along dimension 0, may hold values from -3 to 3
- weights: float32 [256, 256], replicated, may hold values from 0.1 to 1
- counts: int32 [8, 2], P(('grp', 'row'), 'col'), parts along dimension 0, may hold values from 1 to 2, as said below
- offsets: int32 [8, 2, 2, 2], P(('grp', 'row'), 'col'), parts along dimension 0, may hold values from 0 to 383, as said below
- intensities: bfloat16 [8, 2, 2, 256, 256], P(('grp', 'row'), 'col'), parts along dimension 0, may hold values from 0.049804688 to 2
Outputs:
- gradient: float32 [2, 2, 3072, 768], P('slc', None, ('grp', 'row'), 'col'), parts along dimension 2
There are 2 independent parts, one for each index of `grp`. A program takes and returns all parts, laid end to end along the dimension named above; an argument that names none is the same for every part. Nothing has to cross between parts.
Inputs may be any that keep to these rules, and one draw needn't show every extreme that they name: `counts`: some tile has exactly 2 positions. `offsets`: every window of a live position lies inside the object; entries of slots at or after a tile's count are ignored.
All inputs are finite; a program needn't handle non-finite values.
Results may differ from a plain program's by a relative error of at most 0.019.
Values may be sent and summed in bfloat16 or wider, within the bound.
No kernel may reach another device: no remote copies, remote signals or barrier semaphores. Data moves between devices by JAX's collectives and lax.ppermute only.
A program may use at most 64 MiB of HBM per device.

v0:
```python
import jax
import jax.numpy as jnp
from jax import lax
from jax.sharding import PartitionSpec as P

fresnel = 0.5


def from_behind(x, axis, by):
    count = lax.axis_size(axis)
    pairs = [(i, i + by) for i in range(count) if 0 <= i + by < count]
    return lax.ppermute(x, axis, pairs)


def dft_tables(extent):
    counter = jnp.arange(extent, dtype=jnp.int32)
    product = counter[:, None] * counter[None, :] % extent
    angles = 2.0 * jnp.pi / extent * product.astype(jnp.float32)
    norm_scale = 1.0 / jnp.sqrt(jnp.asarray(extent, jnp.float32))
    table_re = (jnp.cos(angles) * norm_scale).astype(jnp.bfloat16)
    table_im = (-jnp.sin(angles) * norm_scale).astype(jnp.bfloat16)
    return (table_re, table_im)


def chirp_factor(extent):
    counter = jnp.arange(extent, dtype=jnp.int32)
    signed_freq = (counter + extent // 2) % extent - extent // 2
    squares = (
        signed_freq[:, None] * signed_freq[:, None] + signed_freq[None, :] * signed_freq[None, :]
    )
    angles = -jnp.pi * fresnel / extent * squares.astype(jnp.float32)
    return (jnp.cos(angles), jnp.sin(angles))


def transform(real, imag, table_re, table_im):
    real_half = real.astype(jnp.bfloat16)
    imag_half = imag.astype(jnp.bfloat16)
    mid_re = jnp.dot(table_re, real_half, preferred_element_type=jnp.float32) - jnp.dot(
        table_im, imag_half, preferred_element_type=jnp.float32
    )
    mid_im = jnp.dot(table_re, imag_half, preferred_element_type=jnp.float32) + jnp.dot(
        table_im, real_half, preferred_element_type=jnp.float32
    )
    mid_re = mid_re.astype(jnp.bfloat16)
    mid_im = mid_im.astype(jnp.bfloat16)
    out_re = jnp.dot(mid_re, table_re, preferred_element_type=jnp.float32) - jnp.dot(
        mid_im, table_im, preferred_element_type=jnp.float32
    )
    out_im = jnp.dot(mid_re, table_im, preferred_element_type=jnp.float32) + jnp.dot(
        mid_im, table_re, preferred_element_type=jnp.float32
    )
    return (out_re, out_im)


def complex_mul(left_re, left_im, right_re, right_im):
    return (left_re * right_re - left_im * right_im, left_re * right_im + left_im * right_re)


def conj_mul(left_re, left_im, right_re, right_im):
    return (left_re * right_re + left_im * right_im, left_re * right_im - left_im * right_re)


def forward_mode(probe_re, probe_im, window, tables, chirps):
    table_re, table_im, inverse_im = tables
    chirp_re, chirp_im = chirps
    first_re = window[0, 0].astype(jnp.float32)
    first_im = window[0, 1].astype(jnp.float32)
    second_re = window[1, 0].astype(jnp.float32)
    second_im = window[1, 1].astype(jnp.float32)
    psi_re, psi_im = complex_mul(probe_re, probe_im, first_re, first_im)
    spec_re, spec_im = transform(psi_re, psi_im, table_re, table_im)
    spec_re, spec_im = complex_mul(chirp_re, chirp_im, spec_re, spec_im)
    prop_re, prop_im = transform(spec_re, spec_im, table_re, inverse_im)
    exit_re, exit_im = complex_mul(prop_re, prop_im, second_re, second_im)
    far_re, far_im = transform(exit_re, exit_im, table_re, table_im)
    return (prop_re, prop_im, far_re, far_im)


def backward_mode(
    probe_re, probe_im, window, prop_re, prop_im, far_re, far_im, residual, tables, chirps
):
    table_re, table_im, inverse_im = tables
    chirp_re, chirp_im = chirps
    second_re = window[1, 0].astype(jnp.float32)
    second_im = window[1, 1].astype(jnp.float32)
    back_re, back_im = transform(residual * far_re, residual * far_im, table_re, inverse_im)
    grad_two_re, grad_two_im = conj_mul(prop_re, prop_im, back_re, back_im)
    gprop_re, gprop_im = conj_mul(second_re, second_im, back_re, back_im)
    gspec_re, gspec_im = transform(gprop_re, gprop_im, table_re, table_im)
    gspec_re, gspec_im = conj_mul(chirp_re, chirp_im, gspec_re, gspec_im)
    gpsi_re, gpsi_im = transform(gspec_re, gspec_im, table_re, inverse_im)
    grad_one_re, grad_one_im = conj_mul(probe_re, probe_im, gpsi_re, gpsi_im)
    return jnp.stack([jnp.stack([grad_one_re, grad_one_im]), jnp.stack([grad_two_re, grad_two_im])])


def body(objects, probes, weights, counts, offsets, intensities):
    slices = objects.shape[0]
    tile_size = objects.shape[2]
    extent = probes.shape[2]
    table_re, table_im = dft_tables(extent)
    tables = (table_re, table_im, -table_im)
    chirps = chirp_factor(extent)
    probe_re = probes[0, 0].astype(jnp.float32)
    probe_im = probes[0, 1].astype(jnp.float32)
    from_right = from_behind(objects[:, :, :, :extent], "col", -1)
    widened = jnp.concatenate([objects, from_right], axis=3)
    from_below = from_behind(widened[:, :, :extent, :], "row", -1)
    extended = jnp.concatenate([widened, from_below], axis=2)
    tile_count = counts[0, 0]
    offset_list = offsets[0, 0]
    measured = intensities[0, 0]
    slot_limit = offset_list.shape[0]
    anchor = jnp.int32(0)

    def slot_gradient(window, data_slot):
        prop_re, prop_im, far_re, far_im = forward_mode(probe_re, probe_im, window, tables, chirps)
        intensity = lax.psum(
            (far_re * far_re + far_im * far_im).astype(jnp.bfloat16), "slc"
        ).astype(jnp.float32)
        residual = 2.0 * weights * (intensity - data_slot.astype(jnp.float32))
        return backward_mode(
            probe_re, probe_im, window, prop_re, prop_im, far_re, far_im, residual, tables, chirps
        )

    def window_at(slot_id):
        corner = offset_list[slot_id]
        return lax.dynamic_slice(
            extended, (anchor, anchor, corner[0], corner[1]), (slices, 2, extent, extent)
        )

    def add_at(gradient, slot_id, contrib):
        corner = offset_list[slot_id]
        start = (anchor, anchor, corner[0], corner[1])
        previous = lax.dynamic_slice(gradient, start, (slices, 2, extent, extent))
        return lax.dynamic_update_slice(gradient, previous + contrib, start)

    gradient = jnp.zeros(extended.shape, jnp.float32)

    def own_step(slot_id, gradient_now):
        contrib = slot_gradient(window_at(slot_id), measured[slot_id])
        contrib = jnp.where(slot_id < tile_count, contrib, jnp.zeros_like(contrib))
        return add_at(gradient_now, slot_id, contrib)

    gradient = lax.fori_loop(0, slot_limit, own_step, gradient)
    share = lax.psum_scatter(
        gradient.astype(jnp.bfloat16), "slc", scatter_dimension=0, tiled=True
    ).astype(jnp.float32)
    from_above = from_behind(share[:, :, tile_size:, :].astype(jnp.bfloat16), "row", 1).astype(
        jnp.float32
    )
    share = jnp.concatenate(
        [share[:, :, :extent, :] + from_above, share[:, :, extent:tile_size, :]], axis=2
    )
    from_left = from_behind(share[:, :, :, tile_size:].astype(jnp.bfloat16), "col", 1).astype(
        jnp.float32
    )
    return jnp.concatenate(
        [share[:, :, :, :extent] + from_left, share[:, :, :, extent:tile_size]], axis=3
    )


def solution(mesh):
    in_specs = (
        P(None, None, ("grp", "row"), "col"),
        P(("grp", "slc"), None, None, None),
        P(),
        P(("grp", "row"), "col"),
        P(("grp", "row"), "col", None, None),
        P(("grp", "row"), "col", None, None, None),
    )
    out_specs = P("slc", None, ("grp", "row"), "col")
    return jax.shard_map(body, mesh=mesh, in_specs=in_specs, out_specs=out_specs, check_vma=False)
```

profile of v0, /device:TPU:10, one launch (start us, length us, event | category | flops | bytes accessed | tf_op | source)
XLA Modules:
  0.0 331.8 jit_solution(6804542011698405931)
XLA Ops:
  8.7 2.5 collective-permute-start
  11.3 16.6 %collective-permute-done = bf16[2,2,384,256]{3,2,1,0:T(8,128)(2,1)S(1)} collective-permute-done((bf16[2,2,384,256]{3,2,1,0:T(8,128)(2,1)S(1)}, bf16[2,2,384,256]{3,2,1,0:T(8,128)(2,1)S(1)}, u32[]{:S(2)}, u32[]{:S(2)}) %collective-permute-start) | collective-permute-done | bytes 786464 | tf_op jit(solution)/shard_map/ppermute | solution.py:12
  29.1 1.9 collective-permute-start.1
  31.1 29.9 %collective-permute-done.1 = bf16[2,2,256,640]{3,2,1,0:T(8,128)(2,1)} collective-permute-done((bf16[2,2,256,640]{3,2,1,0:T(8,128)(2,1)}, bf16[2,2,256,640]{3,2,1,0:T(8,128)(2,1)}, u32[]{:S(2)}, u32[]{:S(2)}) %collective-permute-start.1) | collective-permute-done | bytes 1310752 | tf_op jit(solution)/shard_map/ppermute | solution.py:12
  61.0 3.3 %pad_maximum_fusion = bf16[2,2,640,640]{3,2,1,0:T(8,128)(2,1)} fusion(bf16[2,2,256,640]{3,2,1,0:T(8,128)(2,1)} %collective-permute-done.1, bf16[2,2,384,640]{3,2,1,0:T(8,128)(2,1)S(1)} %constant_dynamic-update-slice_fusion), kind=kLoop, calls=%fused_computation.378 | loop fusion | flops 6553600 | bytes 6553600 | tf_op jit(solution)/shard_map/concatenate | solution.py:108
  64.3 3.1 broadcast_in_dim.2
  67.5 205.3 %while.16 = (s32[]{:T(128)}, f32[2,2,640,640]{3,2,1,0:T(8,128)}, s32[2,2]{1,0:T(2,128)S(1)}, s32[]{:T(128)}, bf16[2,2,640,640]{3,2,1,0:T(8,128)(2,1)}, /*index=5...) while((s32[]{:T(128)}, f32[2,2,640,640]{3,2,1,0:T(8,128)}, ...), condition=%wide.region_2.3_spmd.clone.clone.clone, body=%wide.region_0.2_spmd.clone.clone.clone.sunk | while | flops 1673396224 | bytes 38406500 | solution.py:144
  81.6 2.0 fusion.569
  92.3 2.2 fusion.576
  105.2 18.9 %all-reduce.2.cloned.1.call-done = bf16[256,256]{1,0:T(8,128)(2,1)} async-done(((bf16[256,256]{1,0:T(8,128)(2,1)}), bf16[256,256]{1,0:T(8,128)(2,1)}) %all-reduce.2.cloned.1.call-update) | async-done | bytes 131088 | tf_op jit(solution)/shard_map/while/body/eval_jaxpr/psum | solution.py:117
  133.0 2.5 fusion.589
  143.6 2.0 fusion.596
  157.2 12.4 %dynamic_update_slice.11 = f32[2,2,640,640]{3,2,1,0:T(8,128)} dynamic-update-slice(f32[2,2,640,640]{3,2,1,0:T(8,128)} %get-tuple-element.705, f32[2,2,256,256]{3,2,1,0:T(8,128)S(1)} %fusion.603, s32[]{:T(128)} %constant.69.clone.1..sunk, s32[]{:T(128)} %constant.69.clone.1..sunk, s32[]{:T(128)S(6)} %select_n.381, s32[]{:T(128)S(6)} %select_n.382) | dynamic-update-slice | bytes 2097156 | tf_op jit(solution)/shard_map/while/body/eval_jaxpr/dynamic_update_slice | solution.py:135
  183.6 2.0 fusion.569
  194.1 2.2 fusion.576
  207.0 18.6 %all-reduce.2.cloned.1.call-done = bf16[256,256]{1,0:T(8,128)(2,1)} async-done(((bf16[256,256]{1,0:T(8,128)(2,1)}), bf16[256,256]{1,0:T(8,128)(2,1)}) %all-reduce.2.cloned.1.call-update) | async-done | bytes 131088 | tf_op jit(solution)/shard_map/while/body/eval_jaxpr/psum | solution.py:117
  234.6 2.5 fusion.589
  245.2 2.0 fusion.596
  258.8 12.1 %dynamic_update_slice.11 = f32[2,2,640,640]{3,2,1,0:T(8,128)} dynamic-update-slice(f32[2,2,640,640]{3,2,1,0:T(8,128)} %get-tuple-element.705, f32[2,2,256,256]{3,2,1,0:T(8,128)S(1)} %fusion.603, s32[]{:T(128)} %constant.69.clone.1..sunk, s32[]{:T(128)} %constant.69.clone.1..sunk, s32[]{:T(128)S(6)} %select_n.381, s32[]{:T(128)S(6)} %select_n.382) | dynamic-update-slice | bytes 2097156 | tf_op jit(solution)/shard_map/while/body/eval_jaxpr/dynamic_update_slice | solution.py:135
  272.8 4.9 %convert_element_type.492 = bf16[2,2,640,640]{3,2,1,0:T(8,128)(2,1)} convert(f32[2,2,640,640]{3,2,1,0:T(8,128)} %get-tuple-element.387) | non-fusion elementwise | flops 1638400 | bytes 9830400 | tf_op jit(solution)/shard_map/convert_element_type | solution.py:146
  277.8 12.9 %reduce-scatter.2.cloned.1.call-done = bf16[1,2,640,640]{3,2,1,0:T(8,128)(2,1)} async-done(((bf16[2,2,640,640]{3,2,1,0:T(8,128)(2,1)}), bf16[1,2,640,640]{3,2,1,0:T(8,128)(2,1)}) %reduce-scatter.2.cloned.1.call-update) | async-done | bytes 1638416 | tf_op jit(solution)/shard_map/reduce_scatter | solution.py:145
  292.0 3.4 %collective-permute-start.2 = (bf16[1,2,256,640]{3,2,1,0:T(8,128)(2,1)S(1)}, bf16[1,2,256,640]{3,2,1,0:T(8,128)(2,1)S(1)}, u32[]{:S(2)}, u32[]{:S(2)}) collective-permute-start(bf16[1,2,256,640]{3,2,1,0:T(8,128)(2,1)S(1)} %slice.110), channel_id=1, source_target_pairs={{0,4},{4,8},{8,12},{1,5},{5,9},{9,13},{2,6},{6,10},{10,14},{3,7},{... | collective-permute-start | bytes 1966088 | tf_op jit(solution)/shard_map/ppermute | solution.py:12
  296.6 14.0 %collective-permute-done.2 = bf16[1,2,256,640]{3,2,1,0:T(8,128)(2,1)S(1)} collective-permute-done((bf16[1,2,256,640]{3,2,1,0:T(8,128)(2,1)S(1)}, bf16[1,2,256,640]{3,2,1,0:T(8,128)(2,1)S(1)}, u32[]{:S(2)}, u32[]{:S(2)}) %collective-permute-start.2) | collective-permute-done | bytes 655392 | tf_op jit(solution)/shard_map/ppermute | solution.py:12
  312.1 10.9 %collective-permute-done.3 = bf16[1,2,384,256]{3,2,1,0:T(8,128)(2,1)S(1)} collective-permute-done((bf16[1,2,384,256]{3,2,1,0:T(8,128)(2,1)S(1)}, bf16[1,2,384,256]{3,2,1,0:T(8,128)(2,1)S(1)}, u32[]{:S(2)}, u32[]{:S(2)}) %collective-permute-start.3) | collective-permute-done | bytes 393248 | tf_op jit(solution)/shard_map/ppermute | solution.py:12
  (132 shorter events, 121.2 us)
Async XLA Ops:
  7.4 3.8 %copy-start.2 = (bf16[2,2,384,384]{3,2,1,0:T(8,128)(2,1)S(1)}, bf16[2,2,384,384]{3,2,1,0:T(8,128)(2,1)}, u32[]{:S(2)}) copy-start(bf16[2,2,384,384]{3,2,1,0:T(8,128)(2,1)} %param.8) | copy-start | bytes 3538948
  8.7 19.2 %collective-permute-start = (bf16[2,2,384,256]{3,2,1,0:T(8,128)(2,1)S(1)}, bf16[2,2,384,256]{3,2,1,0:T(8,128)(2,1)S(1)}, u32[]{:S(2)}, u32[]{:S(2)}) collective-permute-start(bf16[2,2,384,256]{3,2,1,0:T(8,128)(2,1)S(1)} %slice.80), channel_id=1, source_target_pairs={{2,0},{3,1},{6,4},{7,5},{10,8},{11,9},{14,12},{15,13},{18,16},{19,... | collective-permute-start | bytes 2359304 | tf_op jit(solution)/shard_map/ppermute | solution.py:12
  11.3 19.8 %copy-start.4 = (bf16[1,2,256,256]{3,2,1,0:T(8,128)(2,1)S(1)}, bf16[1,2,256,256]{3,2,1,0:T(8,128)(2,1)}, u32[]{:S(2)}) copy-start(bf16[1,2,256,256]{3,2,1,0:T(8,128)(2,1)} %param.9) | copy-start | bytes 786436
  29.1 31.9 %collective-permute-start.1 = (bf16[2,2,256,640]{3,2,1,0:T(8,128)(2,1)}, bf16[2,2,256,640]{3,2,1,0:T(8,128)(2,1)}, u32[]{:S(2)}, u32[]{:S(2)}) collective-permute-start(bf16[2,2,256,640]{3,2,1,0:T(8,128)(2,1)} %slice.108), channel_id=1, source_target_pairs={{4,0},{8,4},{12,8},{5,1},{9,5},{13,9},{6,2},{10,6},{14,10},{7,3},{... | collective-permute-start | bytes 3932168 | tf_op jit(solution)/shard_map/ppermute | solution.py:12
  64.3 3.1 copy-start
  64.3 3.1 copy-start.3
  64.3 3.1 copy-start.5
  67.7 56.4 %all-reduce.2.cloned.1.call-start = ((), (), s32[]{:S(2)}) async-start(), calls=%async_computation.2 | async-start | bytes 262144 | tf_op jit(solution)/shard_map/while/body/eval_jaxpr/psum | solution.py:117
  169.7 55.9 %all-reduce.2.cloned.1.call-start = ((), (), s32[]{:S(2)}) async-start(), calls=%async_computation.2 | async-start | bytes 262144 | tf_op jit(solution)/shard_map/while/body/eval_jaxpr/psum | solution.py:117
  272.8 18.0 %reduce-scatter.2.cloned.1.call-start = ((), (), s32[]{:S(2)}) async-start(), calls=%async_computation.1 | async-start | bytes 4915200 | tf_op jit(solution)/shard_map/reduce_scatter | solution.py:145
  290.7 5.7 %copy-start.1 = (bf16[1,2,640,640]{3,2,1,0:T(8,128)(2,1)S(1)}, bf16[1,2,640,640]{3,2,1,0:T(8,128)(2,1)}, u32[]{:S(2)}) copy-start(bf16[1,2,640,640]{3,2,1,0:T(8,128)(2,1)} %reduce-scatter.2.cloned.1.call-done) | copy-start | bytes 4915204
  292.0 18.6 %collective-permute-start.2 = (bf16[1,2,256,640]{3,2,1,0:T(8,128)(2,1)S(1)}, bf16[1,2,256,640]{3,2,1,0:T(8,128)(2,1)S(1)}, u32[]{:S(2)}, u32[]{:S(2)}) collective-permute-start(bf16[1,2,256,640]{3,2,1,0:T(8,128)(2,1)S(1)} %slice.110), channel_id=1, source_target_pairs={{0,4},{4,8},{8,12},{1,5},{5,9},{9,13},{2,6},{6,10},{10,14},{3,7},{... | collective-permute-start | bytes 1966088 | tf_op jit(solution)/shard_map/ppermute | solution.py:12
  310.8 12.2 %collective-permute-start.3 = (bf16[1,2,384,256]{3,2,1,0:T(8,128)(2,1)S(1)}, bf16[1,2,384,256]{3,2,1,0:T(8,128)(2,1)S(1)}, u32[]{:S(2)}, u32[]{:S(2)}) collective-permute-start(bf16[1,2,384,256]{3,2,1,0:T(8,128)(2,1)S(1)} %fusion.339), channel_id=1, source_target_pairs={{0,2},{1,3},{4,6},{5,7},{8,10},{9,11},{12,14},{13,15},{16,18},{17,... | collective-permute-start | bytes 1179656 | tf_op jit(solution)/shard_map/ppermute | solution.py:12
Sparse Core Ops, SparseCore 0:
  104.7 19.3 all-reduce.1
  206.5 19.1 all-reduce.1
Sparse Core Ops, SparseCore 1:
  277.9 12.8 reduce-scatter.1
where the time goes:
time: 335 us; the launch traced here: 332 us
  waiting for transfers between devices  122 us (36%)
  matrix products  121 us (36%)
  local copies, waits for them, and re-layouts  33.7 us (10%)
  other arithmetic  18.1 us (5%)
  between operations  15.2 us (5%)
  loops' own time  12.4 us (4%)
  starting transfers between devices  9.21 us (3%)
    ppermute x4, waiting for transfers between devices, from_behind(): return lax.ppermute(x, axis, pairs)  71.3 us
    psum x2, waiting for transfers between devices, slot_gradient(): lax.psum((far_re * far_re + far_im * far_im).astype(jnp.bfloat16), 'slc')  37.5 us
    dynamic_update_slice x2, local copies, waits for them, and re-layouts, add_at(): return lax.dynamic_update_slice(gradient, previous + contrib, start)  24.4 us
    dot_general x12, matrix products, transform(): jnp.dot(mid_im, table_im, preferred_element_type=jnp.float32)  20.2 us
    dot_general x12, matrix products, transform(): jnp.dot(mid_im, table_re, preferred_element_type=jnp.float32)  17.2 us
    dot_general x12, matrix products, transform(): jnp.dot(table_im, imag_half, preferred_element_type=jnp.float32)  15.5 us
    dot_general x12, matrix products, transform(): jnp.dot(table_im, real_half, preferred_element_type=jnp.float32)  14.1 us
    dot_general x12, matrix products, transform(): jnp.dot(mid_re, table_im, preferred_element_type=jnp.float32)  13.7 us
  transfers between devices with their start and end apart: 7, of which 7 were waited for; matrix products, arithmetic and copies ran while one was open for 0% of the time, Pallas kernels for 0%

commit v1 on v0

v1 whole, which is shorter than its diff:
```python
import functools

import jax
import jax.numpy as jnp
import numpy as np
from jax import lax
from jax.experimental import pallas as pl
from jax.experimental.pallas import tpu as pltpu
from jax.sharding import PartitionSpec as P

fresnel = 0.5
VMEM = pl.BlockSpec(memory_space=pltpu.VMEM)
SMEM = pl.BlockSpec(memory_space=pltpu.SMEM)
PARAMS = pltpu.CompilerParams(vmem_limit_bytes=20 * 2**20)


def host_tables(extent):
    counter = np.arange(extent)
    angles = 2.0 * np.pi / extent * (counter[:, None] * counter[None, :] % extent)
    forward = (np.cos(angles) - 1j * np.sin(angles)) / np.sqrt(extent)
    signed = (counter + extent // 2) % extent - extent // 2
    chirp = np.exp(-1j * np.pi * fresnel / extent * signed * signed)
    carry = (np.conj(forward) * chirp[None, :]) @ forward
    parts = [carry.real, carry.imag, -carry.imag, forward.real, forward.imag, -forward.imag]
    return jnp.asarray(np.stack(parts).astype(np.float32)).astype(jnp.bfloat16)


def dot(left, right):
    return jnp.dot(left, right, preferred_element_type=jnp.float32)


def one_hot(shape, row_sign, offset):
    row = lax.broadcasted_iota(jnp.int32, shape, 0)
    col = lax.broadcasted_iota(jnp.int32, shape, 1)
    return jnp.where((row - col) * row_sign == offset, 1.0, 0.0).astype(jnp.bfloat16)


def cut_kernel(offs, objects, right, below, diag, keep, send):
    me = lax.axis_index("slc")
    tile = objects.shape[2]
    win = diag.shape[1]
    for out, slot in ((send, 1 - me), (keep, me)):
        top, left = offs[2 * slot], offs[2 * slot + 1]
        rows_own = one_hot((win, tile), -1, top)
        rows_far = one_hot((win, win), -1, top - tile)
        cols_own = one_hot((tile, win), 1, left)
        cols_far = one_hot((win, win), 1, left - tile)
        for part in range(2):
            upper = dot(objects[me, part], cols_own) + dot(right[part], cols_far)
            lower = dot(below[part], cols_own) + dot(diag[part], cols_far)
            window = dot(rows_own, upper.astype(jnp.bfloat16)) + dot(
                rows_far, lower.astype(jnp.bfloat16)
            )
            out[part] = window.astype(jnp.bfloat16)


def transform(real, imag, table_re, table_im, table_in):
    real = real.astype(jnp.bfloat16)
    imag = imag.astype(jnp.bfloat16)
    mid_re = (dot(table_re, real) + dot(table_in, imag)).astype(jnp.bfloat16)
    mid_im = (dot(table_re, imag) + dot(table_im, real)).astype(jnp.bfloat16)
    out_re = dot(mid_re, table_re) + dot(mid_im, table_in)
    out_im = dot(mid_re, table_im) + dot(mid_im, table_re)
    return out_re, out_im


def complex_mul(left_re, left_im, right_re, right_im):
    return (left_re * right_re - left_im * right_im, left_re * right_im + left_im * right_re)


def conj_mul(left_re, left_im, right_re, right_im):
    return (left_re * right_re + left_im * right_im, left_re * right_im - left_im * right_re)


def grad_kernel(
    counts, kept, got, probe_a, probe_b, weights, measured, tables, keep, send, prop, far
):
    me = lax.axis_index("slc")
    carry = (tables[0], tables[1], tables[2])
    carry_conj = (tables[0], tables[2], tables[1])
    fwd = (tables[3], tables[4], tables[5])
    inv = (tables[3], tables[5], tables[4])
    first_mine = me == 0

    def pick(part, flag):
        return jnp.where(flag, kept[part], got[part]).astype(jnp.float32)

    probes = (probe_a, probe_b)
    intensity = None
    for mode, probe in enumerate(probes):
        one_re, one_im = pick(0, first_mine), pick(1, first_mine)
        psi = complex_mul(
            probe[0].astype(jnp.float32), probe[1].astype(jnp.float32), one_re, one_im
        )
        prop_re, prop_im = transform(*psi, *carry)
        prop[mode, 0] = prop_re
        prop[mode, 1] = prop_im
        two_re, two_im = pick(0, ~first_mine), pick(1, ~first_mine)
        leave = complex_mul(prop_re, prop_im, two_re, two_im)
        far_re, far_im = transform(*leave, *fwd)
        far[mode, 0] = far_re
        far[mode, 1] = far_im
        square = far_re * far_re + far_im * far_im
        intensity = square if intensity is None else intensity + square
    residual = 2.0 * weights[...] * (intensity - measured[me].astype(jnp.float32))
    residual = jnp.where(me < counts[0], residual, 0.0)
    one_sum = two_sum = None
    for mode, probe in enumerate(probes):
        back_re, back_im = transform(residual * far[mode, 0], residual * far[mode, 1], *inv)
        two = conj_mul(prop[mode, 0], prop[mode, 1], back_re, back_im)
        two_re, two_im = pick(0, ~first_mine), pick(1, ~first_mine)
        inner = conj_mul(two_re, two_im, back_re, back_im)
        gpsi_re, gpsi_im = transform(*inner, *carry_conj)
        one = conj_mul(probe[0].astype(jnp.float32), probe[1].astype(jnp.float32), gpsi_re, gpsi_im)
        one_sum = one if one_sum is None else (one_sum[0] + one[0], one_sum[1] + one[1])
        two_sum = two if two_sum is None else (two_sum[0] + two[0], two_sum[1] + two[1])
    for part in range(2):
        keep[part] = jnp.where(first_mine, one_sum[part], two_sum[part]).astype(jnp.bfloat16)
        send[part] = jnp.where(first_mine, two_sum[part], one_sum[part]).astype(jnp.bfloat16)


def place_kernel(offs, kept, got, own, right, below, diag):
    me = lax.axis_index("slc")
    tile = own.shape[1]
    win = diag.shape[1]
    rows_own, rows_far, cols_own, cols_far = [], [], [], []
    for slot in (me, 1 - me):
        top, left = offs[2 * slot], offs[2 * slot + 1]
        rows_own.append(one_hot((tile, win), 1, top))
        rows_far.append(one_hot((win, win), 1, top - tile))
        cols_own.append(one_hot((win, tile), -1, left))
        cols_far.append(one_hot((win, win), -1, left - tile))
    for part in range(2):
        parts = (kept[part], got[part])
        upper = [dot(rows_own[n], parts[n]).astype(jnp.bfloat16) for n in range(2)]
        lower = [dot(rows_far[n], parts[n]).astype(jnp.bfloat16) for n in range(2)]
        diag[part] = (dot(lower[0], cols_far[0]) + dot(lower[1], cols_far[1])).astype(jnp.bfloat16)
        below[part] = (dot(lower[0], cols_own[0]) + dot(lower[1], cols_own[1])).astype(jnp.bfloat16)
        right[part] = (dot(upper[0], cols_far[0]) + dot(upper[1], cols_far[1])).astype(jnp.bfloat16)
        own[part] = dot(upper[0], cols_own[0]) + dot(upper[1], cols_own[1])


def join_kernel(own, left, above, diag, out):
    tile = own.shape[1]
    win = diag.shape[1]
    for part in range(2):
        out[0, part, win:, win:] = own[part, win:, win:]
        out[0, part, win:, :win] = own[part, win:, :win] + left[part, win:, :].astype(jnp.float32)
        out[0, part, :win, win:] = own[part, :win, win:] + above[part, :, win:].astype(jnp.float32)
        out[0, part, :win, :win] = (
            own[part, :win, :win]
            + left[part, :win, :].astype(jnp.float32)
            + above[part, :, :win].astype(jnp.float32)
            + diag[part].astype(jnp.float32)
        )


def body(rows, cols, objects, probes, weights, counts, offsets, intensities):
    tile = objects.shape[2]
    win = probes.shape[2]
    half = jnp.bfloat16
    me = lax.axis_index("slc")

    def shift(x, down, across):
        pairs = []
        for r in range(rows):
            for c in range(cols):
                if 0 <= r + down < rows and 0 <= c + across < cols:
                    pairs.append((r * cols + c, (r + down) * cols + c + across))
        return lax.ppermute(x, ("row", "col"), pairs)

    def swap(x):
        return lax.ppermute(x, "slc", [(0, 1), (1, 0)])

    def strip(height, width):
        zero = jnp.int32(0)
        return lax.dynamic_slice(objects, (me, zero, zero, zero), (1, 2, height, width))[0]

    right = shift(strip(tile, win), 0, -1)
    below = shift(strip(win, tile), -1, 0)
    diag = shift(strip(win, win), -1, -1)
    probe = probes[0]
    probe_other = swap(probe)
    offs = offsets.reshape(-1)
    window = jax.ShapeDtypeStruct((2, win, win), half)
    keep, send = pl.pallas_call(
        cut_kernel,
        out_shape=(window, window),
        in_specs=[SMEM] + [VMEM] * 4,
        out_specs=(VMEM, VMEM),
        compiler_params=PARAMS,
        name="cut",
    )(offs, objects, right, below, diag)
    got = swap(send)
    keep, send = pl.pallas_call(
        grad_kernel,
        out_shape=(window, window),
        in_specs=[SMEM] + [VMEM] * 7,
        out_specs=(VMEM, VMEM),
        scratch_shapes=[pltpu.VMEM((2, 2, win, win), jnp.float32)] * 2,
        compiler_params=PARAMS,
        name="grad",
    )(
        counts.reshape(-1),
        keep,
        got,
        probe,
        probe_other,
        weights,
        intensities[0, 0],
        host_tables(win),
    )
    got = swap(send)
    own, right, below, diag = pl.pallas_call(
        place_kernel,
        out_shape=(
            jax.ShapeDtypeStruct((2, tile, tile), jnp.float32),
            jax.ShapeDtypeStruct((2, tile, win), half),
            jax.ShapeDtypeStruct((2, win, tile), half),
            window,
        ),
        in_specs=[SMEM] + [VMEM] * 2,
        out_specs=(VMEM,) * 4,
        compiler_params=PARAMS,
        name="place",
    )(offs, keep, got)
    from_left = shift(right, 0, 1)
    from_above = shift(below, 1, 0)
    from_diag = shift(diag, 1, 1)
    return pl.pallas_call(
        join_kernel,
        out_shape=jax.ShapeDtypeStruct((1, 2, tile, tile), jnp.float32),
        in_specs=[VMEM] * 4,
        out_specs=VMEM,
        compiler_params=PARAMS,
        name="join",
    )(own, from_left, from_above, from_diag)


def solution(mesh):
    in_specs = (
        P(None, None, ("grp", "row"), "col"),
        P(("grp", "slc"), None, None, None),
        P(),
        P(("grp", "row"), "col"),
        P(("grp", "row"), "col", None, None),
        P(("grp", "row"), "col", None, None, None),
    )
    out_specs = P("slc", None, ("grp", "row"), "col")
    run = functools.partial(body, mesh.shape["row"], mesh.shape["col"])
    return jax.shard_map(run, mesh=mesh, in_specs=in_specs, out_specs=out_specs, check_vma=False)
```

time: 335 us -> 61.5 us (0.18)
  matrix products: 121 us -> 0 us
  waiting for transfers between devices: 122 us -> 30.4 us
  local copies, waits for them, and re-layouts: 33.7 us -> 4.52 us
  other arithmetic: 18.1 us -> 0 us
  between operations: 15.2 us -> 0.76 us
  loops' own time: 12.4 us -> 0 us
  Pallas kernels: 0 us -> 11.8 us
  starting transfers between devices: 9.21 us -> 13 us
    dot_general x96 -> x0, matrix products: 121 us -> none  [the longest x12 20.2 us: transform(): jnp.dot(mid_im, table_im, preferred_element_type=jnp.float32)]
    ppermute x4 -> x9, waiting for transfers between devices: 71.3 us -> 30.4 us  [the longest x6 28.2 us: shift(): return lax.ppermute(x, ('row', 'col'), pairs)]
    psum x2 -> x0, waiting for transfers between devices: 37.5 us -> none  [slot_gradient(): lax.psum((far_re * far_re + far_im * far_im).astype(jnp.bfloat16), 'slc')]
    dynamic_update_slice x2 -> x0, local copies, waits for them, and re-layouts: 24.4 us -> none  [add_at(): return lax.dynamic_update_slice(gradient, previous + contrib, start)]
    reduce_scatter x1 -> x0, waiting for transfers between devices: 12.9 us -> none  [body(): lax.psum_scatter(gradient.astype(jnp.bfloat16), 'slc', scatter_dimension=...]
    another operation x1 -> x0, loops' own time: 12.4 us -> none  [body(): gradient = lax.fori_loop(0, slot_limit, own_step, gradient)]
    pallas_call x0 -> x4, Pallas kernels: none -> 11.8 us  [the longest x1 4.99 us: body(): pl.pallas_call(grad_kernel, out_shape=(window, window), in_specs=[SMEM] +...]
    convert_element_type x7 -> x0, other arithmetic: 9.61 us -> none  [the longest x1 4.95 us: body(): gradient.astype(jnp.bfloat16)]
  transfers between devices with their start and end apart: 7 -> 9, of which waited for: 7 -> 4; matrix products, arithmetic and copies ran while one was open for 0% -> 4% of each run, Pallas kernels for 0% -> 6%
where the time goes in v1:
time: 61.5 us; the launch traced here: 60.5 us
  waiting for transfers between devices  30.4 us (49%)
  starting transfers between devices  13 us (21%)
  Pallas kernels  11.8 us (19%)
  local copies, waits for them, and re-layouts  4.52 us (7%)
  between operations  0.76 us (1%)
    ppermute x6, waiting for transfers between devices, shift(): return lax.ppermute(x, ('row', 'col'), pairs)  28.2 us
    ppermute x6, starting transfers between devices, shift(): return lax.ppermute(x, ('row', 'col'), pairs)  12.7 us
    pallas_call x1, Pallas kernels, body(): pl.pallas_call(grad_kernel, out_shape=(window, window), in_specs=[SMEM] +...  4.99 us
    squeeze x3, local copies, waits for them, and re-layouts, strip(): lax.dynamic_slice(objects, (me, zero, zero, zero), (1, 2, height, width))[0]  4.41 us
    pallas_call x1, Pallas kernels, body(): pl.pallas_call(cut_kernel, out_shape=(window, window), in_specs=[SMEM] +...  3.36 us
    ppermute x3, waiting for transfers between devices, swap(): return lax.ppermute(x, 'slc', [(0, 1), (1, 0)])  2.27 us
    pallas_call x1, Pallas kernels, body(): pl.pallas_call(place_kernel, out_shape=(jax.ShapeDtypeStruct((2, tile, ti...  2.26 us
  transfers between devices with their start and end apart: 9, of which 4 were waited for; matrix products, arithmetic and copies ran while one was open for 4% of the time, Pallas kernels for 6%

profile of v1, /device:TPU:10, one launch (start us, length us, event | category | flops | bytes accessed | tf_op | source)
XLA Modules:
  0.0 60.5 jit_solution(6686556418069923701)
XLA Ops:
  0.0 1.9 %dynamic-slice_bitcast_fusion.1 = bf16[2,384,256]{2,1,0:T(8,128)(2,1)} fusion(bf16[2,2,384,384]{3,2,1,0:T(8,128)(2,1)} %objects.1, s32[]{:T(128)S(6)} %select_n.2), kind=kLoop, calls=%fused_computation.1 | loop fusion | bytes 786436 | tf_op jit(solution)/shard_map/squeeze | solution.py:177
  1.9 2.5 %collective-permute-start = (bf16[2,384,256]{2,1,0:T(8,128)(2,1)}, bf16[2,384,256]{2,1,0:T(8,128)(2,1)S(1)}, u32[]{:S(2)}, u32[]{:S(2)}) collective-permute-start(bf16[2,384,256]{2,1,0:T(8,128)(2,1)} %dynamic-slice_bitcast_fusion.1), channel_id=1, source_target_pairs={{2,0},{6,4},{10,8},{14,12},{3,1},{7,5},{11,9},{15,13},{18,16},{22,... | collective-permute-start | bytes 1179656 | tf_op jit(solution)/shard_map/ppermute | solution.py:170
  4.4 1.8 %dynamic-slice_bitcast_fusion = bf16[2,256,384]{2,1,0:T(8,128)(2,1)} fusion(bf16[2,2,384,384]{3,2,1,0:T(8,128)(2,1)} %objects.1, s32[]{:T(128)S(6)} %select_n.2), kind=kLoop, calls=%fused_computation | loop fusion | bytes 786436 | tf_op jit(solution)/shard_map/squeeze | solution.py:177
  6.2 1.9 %collective-permute-start.1 = (bf16[2,256,384]{2,1,0:T(8,128)(2,1)}, bf16[2,256,384]{2,1,0:T(8,128)(2,1)S(1)}, u32[]{:S(2)}, u32[]{:S(2)}) collective-permute-start(bf16[2,256,384]{2,1,0:T(8,128)(2,1)} %dynamic-slice_bitcast_fusion), channel_id=1, source_target_pairs={{4,0},{6,2},{8,4},{10,6},{12,8},{14,10},{5,1},{7,3},{9,5},{11,7},{... | collective-permute-start | bytes 1179656 | tf_op jit(solution)/shard_map/ppermute | solution.py:170
  8.1 0.7 %dynamic-slice_bitcast_fusion.2 = bf16[2,256,256]{2,1,0:T(8,128)(2,1)} fusion(bf16[2,2,384,384]{3,2,1,0:T(8,128)(2,1)S(1)} %copy-done, s32[]{:T(128)S(6)} %select_n.2), kind=kLoop, calls=%fused_computation.2 | loop fusion | bytes 524292 | tf_op jit(solution)/shard_map/squeeze | solution.py:177
  8.8 2.1 %collective-permute-start.2 = (bf16[2,256,256]{2,1,0:T(8,128)(2,1)}, bf16[2,256,256]{2,1,0:T(8,128)(2,1)}, u32[]{:S(2)}, u32[]{:S(2)}) collective-permute-start(bf16[2,256,256]{2,1,0:T(8,128)(2,1)} %dynamic-slice_bitcast_fusion.2), channel_id=1, source_target_pairs={{6,0},{10,4},{14,8},{7,1},{11,5},{15,9},{22,16},{26,20},{30,24},{2... | collective-permute-start | bytes 786440 | tf_op jit(solution)/shard_map/ppermute | solution.py:170
  10.9 0.0 collective-permute-start.4
  11.0 0.1 reshape.6.offs
  11.0 11.3 %collective-permute-done.2.diag = bf16[2,256,256]{2,1,0:T(8,128)(2,1)} collective-permute-done((bf16[2,256,256]{2,1,0:T(8,128)(2,1)}, bf16[2,256,256]{2,1,0:T(8,128)(2,1)}, u32[]{:S(2)}, u32[]{:S(2)}) %collective-permute-start.2) | collective-permute-done | bytes 262176 | tf_op jit(solution)/shard_map/ppermute | solution.py:170
  22.4 0.0 collective-permute-done.right
  22.4 0.0 collective-permute-done.1.below
  22.4 3.4 %cut.1 = (bf16[2,256,256]{2,1,0:T(8,128)(2,1)S(1)}, bf16[2,256,256]{2,1,0:T(8,128)(2,1)S(1)}) custom-call(s32[4]{0:T(128)S(1)} %reshape.6.offs, bf16[2,2,384,384]{3,2,1,0:T(8,128)(2,1)S(1)} %copy-done, bf16[2,384,256]{2,1,0:T(8,128)(2,1)S(1)} %collective-permute-done.right, bf16[2,256,384]{2,1,0:T(8,128)(2,1)S(1)} %collective-permute-done.1.below, ...), custom_call_target="tpu_custom_call" | custom-call | tf_op jit(solution)/shard_map/cut/pallas_call | solution.py:186
  25.7 0.1 collective-permute-start.3
  26.4 0.0 collective-permute-done.4.probe_b
  26.5 0.9 %collective-permute-done.3.got = bf16[2,256,256]{2,1,0:T(8,128)(2,1)S(1)} collective-permute-done((bf16[2,256,256]{2,1,0:T(8,128)(2,1)S(1)}, bf16[2,256,256]{2,1,0:T(8,128)(2,1)S(1)}, u32[]{:S(2)}, u32[]{:S(2)}) %collective-permute-start.3) | collective-permute-done | bytes 262176 | tf_op jit(solution)/shard_map/ppermute | solution.py:173
  27.3 5.0 %grad.1 = (bf16[2,256,256]{2,1,0:T(8,128)(2,1)S(1)}, bf16[2,256,256]{2,1,0:T(8,128)(2,1)S(1)}) custom-call(s32[1]{0:T(128)} %bitcast.9.counts, bf16[2,256,256]{2,1,0:T(8,128)(2,1)S(1)} %get-tuple-element.13.kept, bf16[2,256,256]{2,1,0:T(8,128)(2,1)S(1)} %collective-permute-done.3.got, bf16[2,256,256]{2,1,0:T(8,128)(2,1)S(1)} %bitcast.11, ...), custom_call_target="tpu_custom_call" | custom-call | tf_op jit(solution)/shard_map/grad/pallas_call | solution.py:195
  32.3 0.2 collective-permute-start.5
  32.5 1.4 %collective-permute-done.5.got = bf16[2,256,256]{2,1,0:T(8,128)(2,1)S(1)} collective-permute-done((bf16[2,256,256]{2,1,0:T(8,128)(2,1)S(1)}, bf16[2,256,256]{2,1,0:T(8,128)(2,1)S(1)}, u32[]{:S(2)}, u32[]{:S(2)}) %collective-permute-start.5) | collective-permute-done | bytes 262176 | tf_op jit(solution)/shard_map/ppermute | solution.py:173
  33.9 2.3 %place.1 = (f32[2,384,384]{2,1,0:T(8,128)S(1)}, bf16[2,384,256]{2,1,0:T(8,128)(2,1)S(1)}, bf16[2,256,384]{2,1,0:T(8,128)(2,1)S(1)}, bf16[2,256,256]{2,1,0:T(8,128)(2,1)S(1)}) custom-call(s32[4]{0:T(128)S(1)} %reshape.6.offs, bf16[2,256,256]{2,1,0:T(8,128)(2,1)S(1)} %get-tuple-element.15.kept, bf16[2,256,256]{2,1,0:T(8,128)(2,1)S(1)} %collective-permute-done.5.got), custom_call_target="tpu_custom_call" | custom-call | tf_op jit(solution)/shard_map/place/pallas_call | solution.py:214
  36.2 1.3 %collective-permute-start.6 = (bf16[2,384,256]{2,1,0:T(8,128)(2,1)S(1)}, bf16[2,384,256]{2,1,0:T(8,128)(2,1)S(1)}, u32[]{:S(2)}, u32[]{:S(2)}) collective-permute-start(bf16[2,384,256]{2,1,0:T(8,128)(2,1)S(1)} %get-tuple-element.18), channel_id=1, source_target_pairs={{0,2},{4,6},{8,10},{12,14},{1,3},{5,7},{9,11},{13,15},{16,18},{20,... | collective-permute-start | bytes 1179656 | tf_op jit(solution)/shard_map/ppermute | solution.py:170
  37.5 3.6 %collective-permute-start.7 = (bf16[2,256,384]{2,1,0:T(8,128)(2,1)S(1)}, bf16[2,256,384]{2,1,0:T(8,128)(2,1)S(1)}, u32[]{:S(2)}, u32[]{:S(2)}) collective-permute-start(bf16[2,256,384]{2,1,0:T(8,128)(2,1)S(1)} %get-tuple-element.19), channel_id=1, source_target_pairs={{0,4},{2,6},{4,8},{6,10},{8,12},{10,14},{1,5},{3,7},{5,9},{7,11},{... | collective-permute-start | bytes 1179656 | tf_op jit(solution)/shard_map/ppermute | solution.py:170
  41.2 1.3 %collective-permute-start.8 = (bf16[2,256,256]{2,1,0:T(8,128)(2,1)S(1)}, bf16[2,256,256]{2,1,0:T(8,128)(2,1)S(1)}, u32[]{:S(2)}, u32[]{:S(2)}) collective-permute-start(bf16[2,256,256]{2,1,0:T(8,128)(2,1)S(1)} %get-tuple-element.20), channel_id=1, source_target_pairs={{0,6},{4,10},{8,14},{1,7},{5,11},{9,15},{16,22},{20,26},{24,30},{1... | collective-permute-start | bytes 786440 | tf_op jit(solution)/shard_map/ppermute | solution.py:170
  42.5 16.8 %collective-permute-done.8.diag = bf16[2,256,256]{2,1,0:T(8,128)(2,1)S(1)} collective-permute-done((bf16[2,256,256]{2,1,0:T(8,128)(2,1)S(1)}, bf16[2,256,256]{2,1,0:T(8,128)(2,1)S(1)}, u32[]{:S(2)}, u32[]{:S(2)}) %collective-permute-start.8) | collective-permute-done | bytes 262176 | tf_op jit(solution)/shard_map/ppermute | solution.py:170
  59.3 1.2 %join.1 = f32[1,2,384,384]{3,2,1,0:T(8,128)} custom-call(f32[2,384,384]{2,1,0:T(8,128)S(1)} %get-tuple-element.17.own, bf16[2,384,256]{2,1,0:T(8,128)(2,1)S(1)} %collective-permute-done.6.left, bf16[2,256,384]{2,1,0:T(8,128)(2,1)S(1)} %collective-permute-done.7.above, bf16[2,256,256]{2,1,0:T(8,128)(2,1)S(1)} %collective-permute-done.8.diag), custom_call_target="tpu_custom_call" | custom-call | tf_op jit(solution)/shard_map/join/pallas_call | solution.py:230
  (14 shorter events, 0.0 us)
Async XLA Ops:
  0.0 8.1 %copy-start = (bf16[2,2,384,384]{3,2,1,0:T(8,128)(2,1)S(1)}, bf16[2,2,384,384]{3,2,1,0:T(8,128)(2,1)}, u32[]{:S(2)}) copy-start(bf16[2,2,384,384]{3,2,1,0:T(8,128)(2,1)} %objects.1) | copy-start | bytes 3538948
  0.0 10.9 %copy-start.2 = (bf16[1,2,256,256]{3,2,1,0:T(8,128)(2,1)S(1)}, bf16[1,2,256,256]{3,2,1,0:T(8,128)(2,1)}, u32[]{:S(2)}) copy-start(bf16[1,2,256,256]{3,2,1,0:T(8,128)(2,1)} %param.8) | copy-start | bytes 786436
  0.0 10.9 %copy-start.5 = (s32[1,1,2,2]{3,2,1,0:T(2,128)S(1)}, s32[1,1,2,2]{3,2,1,0:T(2,128)}, u32[]{:S(2)}) copy-start(s32[1,1,2,2]{3,2,1,0:T(2,128)} %param.11) | copy-start | bytes 52
  1.9 20.5 %collective-permute-start = (bf16[2,384,256]{2,1,0:T(8,128)(2,1)}, bf16[2,384,256]{2,1,0:T(8,128)(2,1)S(1)}, u32[]{:S(2)}, u32[]{:S(2)}) collective-permute-start(bf16[2,384,256]{2,1,0:T(8,128)(2,1)} %dynamic-slice_bitcast_fusion.1), channel_id=1, source_target_pairs={{2,0},{6,4},{10,8},{14,12},{3,1},{7,5},{11,9},{15,13},{18,16},{22,... | collective-permute-start | bytes 1179656 | tf_op jit(solution)/shard_map/ppermute | solution.py:170
  6.2 16.2 %collective-permute-start.1 = (bf16[2,256,384]{2,1,0:T(8,128)(2,1)}, bf16[2,256,384]{2,1,0:T(8,128)(2,1)S(1)}, u32[]{:S(2)}, u32[]{:S(2)}) collective-permute-start(bf16[2,256,384]{2,1,0:T(8,128)(2,1)} %dynamic-slice_bitcast_fusion), channel_id=1, source_target_pairs={{4,0},{6,2},{8,4},{10,6},{12,8},{14,10},{5,1},{7,3},{9,5},{11,7},{... | collective-permute-start | bytes 1179656 | tf_op jit(solution)/shard_map/ppermute | solution.py:170
  8.8 18.5 %copy-start.1 = (bf16[6,256,256]{2,1,0:T(8,128)(2,1)S(1)}, bf16[6,256,256]{2,1,0:T(8,128)(2,1)}, u32[]{:S(2)}) copy-start(bf16[6,256,256]{2,1,0:T(8,128)(2,1)} %constant.15.tables) | copy-start | bytes 2359300
  8.8 18.5 %copy-start.3 = (f32[256,256]{1,0:T(8,128)S(1)}, f32[256,256]{1,0:T(8,128)}, u32[]{:S(2)}) copy-start(f32[256,256]{1,0:T(8,128)} %weights.1) | copy-start | bytes 786436
  8.8 18.5 %copy-start.4 = (bf16[1,1,2,256,256]{4,3,2,1,0:T(8,128)(2,1)S(1)}, bf16[1,1,2,256,256]{4,3,2,1,0:T(8,128)(2,1)}, u32[]{:S(2)}) copy-start(bf16[1,1,2,256,256]{4,3,2,1,0:T(8,128)(2,1)} %param.12) | copy-start | bytes 786436
  8.8 13.5 %collective-permute-start.2 = (bf16[2,256,256]{2,1,0:T(8,128)(2,1)}, bf16[2,256,256]{2,1,0:T(8,128)(2,1)}, u32[]{:S(2)}, u32[]{:S(2)}) collective-permute-start(bf16[2,256,256]{2,1,0:T(8,128)(2,1)} %dynamic-slice_bitcast_fusion.2), channel_id=1, source_target_pairs={{6,0},{10,4},{14,8},{7,1},{11,5},{15,9},{22,16},{26,20},{30,24},{2... | collective-permute-start | bytes 786440 | tf_op jit(solution)/shard_map/ppermute | solution.py:170
  10.9 15.5 %collective-permute-start.4 = (bf16[2,256,256]{2,1,0:T(8,128)(2,1)S(1)}, bf16[2,256,256]{2,1,0:T(8,128)(2,1)}, u32[]{:S(2)}, u32[]{:S(2)}) collective-permute-start(bf16[2,256,256]{2,1,0:T(8,128)(2,1)S(1)} %bitcast.10), channel_id=1, source_target_pairs={{0,1},{1,0},{2,3},{3,2},{4,5},{5,4},{6,7},{7,6},{8,9},{9,8},{10,11... | collective-permute-start | bytes 786440 | tf_op jit(solution)/shard_map/ppermute | solution.py:173
  25.7 1.6 %collective-permute-start.3 = (bf16[2,256,256]{2,1,0:T(8,128)(2,1)S(1)}, bf16[2,256,256]{2,1,0:T(8,128)(2,1)S(1)}, u32[]{:S(2)}, u32[]{:S(2)}) collective-permute-start(bf16[2,256,256]{2,1,0:T(8,128)(2,1)S(1)} %get-tuple-element.14), channel_id=1, source_target_pairs={{0,1},{1,0},{2,3},{3,2},{4,5},{5,4},{6,7},{7,6},{8,9},{9,8},{10,11... | collective-permute-start | bytes 786440 | tf_op jit(solution)/shard_map/ppermute | solution.py:173
  32.3 1.6 %collective-permute-start.5 = (bf16[2,256,256]{2,1,0:T(8,128)(2,1)S(1)}, bf16[2,256,256]{2,1,0:T(8,128)(2,1)S(1)}, u32[]{:S(2)}, u32[]{:S(2)}) collective-permute-start(bf16[2,256,256]{2,1,0:T(8,128)(2,1)S(1)} %get-tuple-element.16), channel_id=1, source_target_pairs={{0,1},{1,0},{2,3},{3,2},{4,5},{5,4},{6,7},{7,6},{8,9},{9,8},{10,11... | collective-permute-start | bytes 786440 | tf_op jit(solution)/shard_map/ppermute | solution.py:173
  36.2 23.1 %collective-permute-start.6 = (bf16[2,384,256]{2,1,0:T(8,128)(2,1)S(1)}, bf16[2,384,256]{2,1,0:T(8,128)(2,1)S(1)}, u32[]{:S(2)}, u32[]{:S(2)}) collective-permute-start(bf16[2,384,256]{2,1,0:T(8,128)(2,1)S(1)} %get-tuple-element.18), channel_id=1, source_target_pairs={{0,2},{4,6},{8,10},{12,14},{1,3},{5,7},{9,11},{13,15},{16,18},{20,... | collective-permute-start | bytes 1179656 | tf_op jit(solution)/shard_map/ppermute | solution.py:170
  37.5 21.8 %collective-permute-start.7 = (bf16[2,256,384]{2,1,0:T(8,128)(2,1)S(1)}, bf16[2,256,384]{2,1,0:T(8,128)(2,1)S(1)}, u32[]{:S(2)}, u32[]{:S(2)}) collective-permute-start(bf16[2,256,384]{2,1,0:T(8,128)(2,1)S(1)} %get-tuple-element.19), channel_id=1, source_target_pairs={{0,4},{2,6},{4,8},{6,10},{8,12},{10,14},{1,5},{3,7},{5,9},{7,11},{... | collective-permute-start | bytes 1179656 | tf_op jit(solution)/shard_map/ppermute | solution.py:170
  41.2 18.1 %collective-permute-start.8 = (bf16[2,256,256]{2,1,0:T(8,128)(2,1)S(1)}, bf16[2,256,256]{2,1,0:T(8,128)(2,1)S(1)}, u32[]{:S(2)}, u32[]{:S(2)}) collective-permute-start(bf16[2,256,256]{2,1,0:T(8,128)(2,1)S(1)} %get-tuple-element.20), channel_id=1, source_target_pairs={{0,6},{4,10},{8,14},{1,7},{5,11},{9,15},{16,22},{20,26},{24,30},{1... | collective-permute-start | bytes 786440 | tf_op jit(solution)/shard_map/ppermute | solution.py:170

commit v2 on v1

v2 whole, which is shorter than its diff:
```python
import functools

import jax
import jax.numpy as jnp
import numpy as np
from jax import lax
from jax.experimental import pallas as pl
from jax.experimental.pallas import tpu as pltpu
from jax.sharding import PartitionSpec as P


fresnel = 0.5
VMEM = pl.BlockSpec(memory_space=pltpu.VMEM)
HBM = pl.BlockSpec(memory_space=pltpu.HBM)
SMEM = pl.BlockSpec(memory_space=pltpu.SMEM)
PARAMS = pltpu.CompilerParams(vmem_limit_bytes=20 * 2**20)


def host_tables(extent):
    counter = np.arange(extent)
    angles = 2.0 * np.pi / extent * (counter[:, None] * counter[None, :] % extent)
    forward = (np.cos(angles) - 1j * np.sin(angles)) / np.sqrt(extent)
    signed = (counter + extent // 2) % extent - extent // 2
    chirp = np.exp(-1j * np.pi * fresnel / extent * signed * signed)
    carry = (np.conj(forward) * chirp[None, :]) @ forward
    parts = [carry.real, carry.imag, -carry.imag, forward.real, forward.imag, -forward.imag]
    return jnp.asarray(np.stack(parts).astype(np.float32)).astype(jnp.bfloat16)


def dot(left, right):
    return jnp.dot(left, right, preferred_element_type=jnp.float32)


def one_hot(shape, row_sign, offset):
    row = lax.broadcasted_iota(jnp.int32, shape, 0)
    col = lax.broadcasted_iota(jnp.int32, shape, 1)
    return jnp.where((row - col) * row_sign == offset, 1.0, 0.0).astype(jnp.bfloat16)


def strip_moves(tile, win):
    half, rest = win // 2, tile - win
    right = (
        (0, 0, 0, half, win, half, 0),
        (1, 0, 0, half, win, 0, 0),
        (1, half, 0, rest, win, win, 0),
    )
    below = (
        (0, 0, 0, half, win, 0, 0),
        (1, 0, 0, half, win, half, 0),
        (1, half, 0, half, rest, 0, win),
        (1, half, rest, half, rest, half, win),
    )
    return right, below


def by_core(me, run):
    for core in range(2):

        @pl.when(me == core)
        def _(core=core):
            run(core)


def strips_kernel(objects, one, two, sems):
    me = lax.axis_index("slc")
    tile = objects.shape[2]
    win = two.shape[2]

    def run(core):
        copies = []
        for move in strip_moves(tile, win)[core]:
            out, row, col, height, width, from_row, from_col = move
            copies.append(
                pltpu.make_async_copy(
                    objects.at[:, :, pl.ds(from_row, height), pl.ds(from_col, width)],
                    (one, two)[out].at[:, :, pl.ds(row, height), pl.ds(col, width)],
                    sems.at[len(copies)],
                )
            )
        for copy in copies:
            copy.start()
        for copy in copies:
            copy.wait()

    by_core(me, run)


def half_of(value):
    return value.astype(jnp.bfloat16)


def prepare_kernel(offs, objects, tall, wide, held):
    me = lax.axis_index("slc")
    tile = objects.shape[2]
    ext, win = tall.shape[2:]
    for n, slot in enumerate((me, 1 - me)):
        for dim in range(2):
            offset = offs[2 * slot + dim]
            tall[n, dim] = one_hot((ext, win), 1, offset)
            wide[n, dim] = one_hot((win, ext), -1, offset)
    for k in range(2):
        for part in range(2):
            upper = half_of(dot(objects[k, part], tall[0, 1, :tile]))
            held[k, part] = half_of(dot(wide[0, 0, :, :tile], upper))


def reach_kernel(tall, wide, held, one, two, out):
    me = lax.axis_index("slc")
    half, win = one.shape[2:]
    tile = tall.shape[2] - win
    rest = tile - win

    def run(core):
        for k in range(2):
            for part in range(2):
                first = one[k, part]
                second = two.at[k, part]
                if core == 0:
                    got = jnp.concatenate([second[:half], first, second[half:]], axis=0)
                else:
                    near = jnp.concatenate([first, second[:half]], axis=0)
                    side = jnp.concatenate([second[half:, :rest], second[half:, rest:]], axis=0)
                    got = jnp.concatenate([near, side], axis=1)
                for n in range(2):
                    if core == 0:
                        window = dot(wide[n, 0, :, :tile], half_of(dot(got, tall[n, 1, tile:])))
                    else:
                        window = dot(wide[n, 0, :, tile:], half_of(dot(got, tall[n, 1, :tile])))
                    if n == 0:
                        window = held[k, part].astype(jnp.float32) + window
                    out[n, k, part] = half_of(window)

    by_core(me, run)


def corner_kernel(tall, wide, held, three, keep, send):
    me = lax.axis_index("slc")
    half, win = three.shape[2:]
    tile = tall.shape[2] - win

    def run(core):
        start = tile + half * (1 - core)
        for n, out in ((1, send), (0, keep)):
            for k in range(2):
                for part in range(2):
                    lower = half_of(dot(three[k, part], tall[n, 1, tile:]))
                    window = dot(wide[n, 0, :, start : start + half], lower)
                    out[k, part] = half_of(held[n, k, part].astype(jnp.float32) + window)

    by_core(me, run)


def transform(real, imag, table_re, table_im, table_in):
    real = real.astype(jnp.bfloat16)
    imag = imag.astype(jnp.bfloat16)
    mid_re = (dot(table_re, real) + dot(table_in, imag)).astype(jnp.bfloat16)
    mid_im = (dot(table_re, imag) + dot(table_im, real)).astype(jnp.bfloat16)
    out_re = dot(mid_re, table_re) + dot(mid_im, table_in)
    out_im = dot(mid_re, table_im) + dot(mid_im, table_re)
    return out_re, out_im


def complex_mul(left_re, left_im, right_re, right_im):
    return (left_re * right_re - left_im * right_im, left_re * right_im + left_im * right_re)


def conj_mul(left_re, left_im, right_re, right_im):
    return (left_re * right_re + left_im * right_im, left_re * right_im - left_im * right_re)


def grad_kernel(
    counts, kept, got, probe_a, probe_b, weights, measured, tables, out, objs, prop, far
):
    me = lax.axis_index("slc")
    carry = (tables[0], tables[1], tables[2])
    carry_conj = (tables[0], tables[2], tables[1])
    fwd = (tables[3], tables[4], tables[5])
    inv = (tables[3], tables[5], tables[4])
    full = jnp.float32
    for k in range(2):
        for part in range(2):
            objs[k, part] = kept[k, part].astype(full) + got[k, part].astype(full)
    probes = (probe_a, probe_b)
    intensity = None
    for mode, probe in enumerate(probes):
        psi = complex_mul(probe[0].astype(full), probe[1].astype(full), objs[0, 0], objs[0, 1])
        prop_re, prop_im = transform(*psi, *carry)
        prop[mode, 0] = prop_re
        prop[mode, 1] = prop_im
        leave = complex_mul(prop_re, prop_im, objs[1, 0], objs[1, 1])
        far_re, far_im = transform(*leave, *fwd)
        far[mode, 0] = far_re
        far[mode, 1] = far_im
        square = far_re * far_re + far_im * far_im
        intensity = square if intensity is None else intensity + square
    residual = 2.0 * weights[...] * (intensity - measured[me].astype(full))
    residual = jnp.where(me < counts[0], residual, 0.0)
    one_sum = two_sum = None
    for mode, probe in enumerate(probes):
        back_re, back_im = transform(residual * far[mode, 0], residual * far[mode, 1], *inv)
        two = conj_mul(prop[mode, 0], prop[mode, 1], back_re, back_im)
        inner = conj_mul(objs[1, 0], objs[1, 1], back_re, back_im)
        gpsi_re, gpsi_im = transform(*inner, *carry_conj)
        one = conj_mul(probe[0].astype(full), probe[1].astype(full), gpsi_re, gpsi_im)
        one_sum = one if one_sum is None else (one_sum[0] + one[0], one_sum[1] + one[1])
        two_sum = two if two_sum is None else (two_sum[0] + two[0], two_sum[1] + two[1])
    for part in range(2):
        out[0, part] = half_of(one_sum[part])
        out[1, part] = half_of(two_sum[part])


def placed(tall, wide, grads, k, part, rows, cols):
    total = None
    for n, grad in enumerate(grads):
        left = half_of(dot(tall[n, 0, rows[0] : rows[0] + rows[1]], grad[k, part]))
        term = dot(left, wide[n, 1, :, cols[0] : cols[0] + cols[1]])
        total = term if total is None else total + term
    return total


def tip_kernel(tall, wide, kept, got, one):
    me = lax.axis_index("slc")
    half, win = one.shape[2:]
    tile = tall.shape[2] - win

    def run(core):
        for k in range(2):
            for part in range(2):
                one[k, part] = half_of(
                    placed(
                        tall,
                        wide,
                        (kept, got),
                        k,
                        part,
                        (tile + half * core, half),
                        (tile, win),
                    )
                )

    by_core(me, run)


def side_kernel(tall, wide, kept, got, two, add):
    me = lax.axis_index("slc")
    half, win = add.shape[2:]
    tile = tall.shape[2] - win
    rest = tile - win

    def run(core):
        for k in range(2):
            for part in range(2):
                put = functools.partial(placed, tall, wide, (kept, got), k, part)
                out = two.at[k, part]
                if core == 0:
                    out[:half] = half_of(put((0, half), (tile, win)))
                    out[half:] = half_of(put((win, rest), (tile, win)))
                    add[k, part] = put((tile, half), (0, win))
                else:
                    out[:half] = half_of(put((tile + half, half), (0, win)))
                    side = half_of(put((tile, win), (win, rest)))
                    out[half:, :rest] = side[:half]
                    out[half:, rest:] = side[half:]
                    add[k, part] = put((half, half), (tile, win))

    by_core(me, run)


def add_kernel(mine, got, out):
    out[...] = half_of(mine[...] + got[...].astype(jnp.float32))


def own_kernel(tall, wide, kept, got, own):
    me = lax.axis_index("slc")
    tile = own.shape[1]
    for part in range(2):
        own[part] = placed(tall, wide, (kept, got), me, part, (0, tile), (0, tile))


def join_kernel(own, two_mine, two_other, three_mine, three_other, out):
    me = lax.axis_index("slc")
    half, win = three_mine.shape[2:]
    tile = own.shape[1]
    rest = tile - win
    full = jnp.float32

    def run(core):
        x_two, z_two = (two_mine, two_other) if core == 0 else (two_other, two_mine)
        z_three, x_three = (three_mine, three_other) if core == 0 else (three_other, three_mine)
        for part in range(2):
            out[0, part, win:, win:] = own[part, win:, win:]
            out[0, part, win:, :win] = own[part, win:, :win] + x_two[core, part, half:].astype(full)
            out[0, part, :half, win:] = own[part, :half, win:] + z_two[
                core, part, half:, :rest
            ].astype(full)
            out[0, part, half:win, win:] = own[part, half:win, win:] + z_two[
                core, part, half:, rest:
            ].astype(full)
            out[0, part, :half, :win] = (
                own[part, :half, :win]
                + x_two[core, part, :half].astype(full)
                + z_three[core, part].astype(full)
            )
            out[0, part, half:win, :win] = (
                own[part, half:win, :win]
                + x_three[core, part].astype(full)
                + z_two[core, part, :half].astype(full)
            )

    by_core(me, run)


def call(kernel, out_shape, *args, specs=None, scratch=()):
    return pl.pallas_call(
        kernel,
        out_shape=out_shape,
        in_specs=specs or [VMEM] * len(args),
        out_specs=jax.tree.map(lambda _: VMEM, out_shape),
        scratch_shapes=scratch,
        compiler_params=PARAMS,
    )(*args)


def body(rows, cols, objects, probes, weights, counts, offsets, intensities):
    tile = objects.shape[2]
    win = probes.shape[2]
    half, ext = win // 2, tile + win
    low = jnp.bfloat16

    def shift(x, step, across):
        pairs = []
        for r in range(rows):
            for c in range(cols):
                for core in range(2):
                    down, over = (0, step) if core == across else (step, 0)
                    if 0 <= r + down < rows and 0 <= c + over < cols:
                        target = (r + down) * cols + c + over
                        pairs.append(((r * cols + c) * 2 + core, target * 2 + core))
        return lax.ppermute(x, ("row", "col", "slc"), pairs)

    def swap(x):
        return lax.ppermute(x, "slc", [(0, 1), (1, 0)])

    def shape(*dims, dtype=low):
        return jax.ShapeDtypeStruct(dims, dtype)

    offs = offsets.reshape(-1)
    quad = shape(2, 2, win, win)
    piece = shape(2, 2, half, win)
    moves = max(len(moves) for moves in strip_moves(tile, win))
    one, two = call(
        strips_kernel,
        (piece, quad),
        objects,
        specs=[HBM],
        scratch=[pltpu.SemaphoreType.DMA((moves,))],
    )
    one = shift(one, -1, 0)
    two = shift(two, -1, 0)
    probe = probes[0]
    probe_other = swap(probe)
    tall, wide, held = call(
        prepare_kernel,
        (shape(2, 2, ext, win), shape(2, 2, win, ext), quad),
        offs,
        objects,
        specs=[SMEM, VMEM],
    )
    three = shift(one, -1, 1)
    held = call(reach_kernel, shape(2, 2, 2, win, win), tall, wide, held, one, two)
    keep, send = call(corner_kernel, (quad, quad), tall, wide, held, three)
    got = swap(send)
    grads = call(
        grad_kernel,
        quad,
        counts.reshape(-1),
        keep,
        got,
        probe,
        probe_other,
        weights,
        intensities[0, 0],
        host_tables(win),
        specs=[SMEM] + [VMEM] * 7,
        scratch=[pltpu.VMEM((2, 2, win, win), jnp.float32)] * 3,
    )
    got = swap(grads)
    one = shift(call(tip_kernel, piece, tall, wide, grads, got), 1, 0)
    addend = shape(2, 2, half, win, dtype=jnp.float32)
    two, add = call(side_kernel, (quad, addend), tall, wide, grads, got)
    two = shift(two, 1, 0)
    three = shift(call(add_kernel, piece, add, one), 1, 1)
    own = call(own_kernel, shape(2, tile, tile, dtype=jnp.float32), tall, wide, grads, got)
    return call(
        join_kernel,
        shape(1, 2, tile, tile, dtype=jnp.float32),
        own,
        two,
        swap(two),
        three,
        swap(three),
    )


def staged(rows, cols, *args):
    return body(rows, cols, *args)


def solution(mesh):
    in_specs = (
        P(None, None, ("grp", "row"), "col"),
        P(("grp", "slc"), None, None, None),
        P(),
        P(("grp", "row"), "col"),
        P(("grp", "row"), "col", None, None),
        P(("grp", "row"), "col", None, None, None),
    )
    out_specs = P("slc", None, ("grp", "row"), "col")
    run = functools.partial(staged, mesh.shape["row"], mesh.shape["col"])
    return jax.shard_map(run, mesh=mesh, in_specs=in_specs, out_specs=out_specs, check_vma=False)
```

time: 61.5 us -> 57.8 us (0.940)
  local copies, waits for them, and re-layouts: 4.52 us -> 1.38 us
  waiting for transfers between devices: 30.4 us -> 29 us
  Pallas kernels: 11.8 us -> 13 us
    squeeze x3 -> x0, local copies, waits for them, and re-layouts: 4.41 us -> none  [strip(): lax.dynamic_slice(objects, (me, zero, zero, zero), (1, 2, height, width))[0]]
    ppermute x6, waiting for transfers between devices: 28.2 us -> 25.6 us  [shift(): return lax.ppermute(x, ('row', 'col', 'slc'), pairs)]
    unnamed x12 -> x14, local copies, waits for them, and re-layouts: 0.02 us -> 1.3 us
    pallas_call x4 -> x10, Pallas kernels: 11.8 us -> 13 us  [call(): pl.pallas_call(kernel, out_shape=out_shape, in_specs=specs or [VMEM] * le...]
    ppermute x3 -> x5, waiting for transfers between devices: 2.27 us -> 3.39 us  [swap(): return lax.ppermute(x, 'slc', [(0, 1), (1, 0)])]
    ppermute x3 -> x5, starting transfers between devices: 0.27 us -> 1.14 us  [swap(): return lax.ppermute(x, 'slc', [(0, 1), (1, 0)])]
    ppermute x6, starting transfers between devices: 12.7 us -> 11.9 us  [shift(): return lax.ppermute(x, ('row', 'col', 'slc'), pairs)]
  transfers between devices with their start and end apart: 9 -> 11, of which waited for: 4 -> 7; matrix products, arithmetic and copies ran while one was open for 4% -> 0% of each run, Pallas kernels for 6% -> 10%
where the time goes in v2:
time: 57.8 us; the launch traced here: 57.2 us
  waiting for transfers between devices  29 us (50%)
  Pallas kernels  13 us (22%)
  starting transfers between devices  13 us (22%)
  local copies, waits for them, and re-layouts  1.38 us (2%)
  between operations  0.84 us (1%)
    ppermute x6, waiting for transfers between devices, shift(): return lax.ppermute(x, ('row', 'col', 'slc'), pairs)  25.6 us
    pallas_call x10, Pallas kernels, call(): pl.pallas_call(kernel, out_shape=out_shape, in_specs=specs or [VMEM] * le...  13 us
    ppermute x6, starting transfers between devices, shift(): return lax.ppermute(x, ('row', 'col', 'slc'), pairs)  11.9 us
    ppermute x5, waiting for transfers between devices, swap(): return lax.ppermute(x, 'slc', [(0, 1), (1, 0)])  3.39 us
    unnamed x14, local copies, waits for them, and re-layouts  1.3 us
  transfers between devices with their start and end apart: 11, of which 7 were waited for; matrix products, arithmetic and copies ran while one was open for 0% of the time, Pallas kernels for 10%

profile of v2, /device:TPU:10, one launch (start us, length us, event | category | flops | bytes accessed | tf_op | source)
XLA Modules:
  0.0 57.2 jit_solution(1163660076475395725)
XLA Ops:
  0.0 1.3 %copy-done = bf16[2,2,384,384]{3,2,1,0:T(8,128)(2,1)S(1)} copy-done((bf16[2,2,384,384]{3,2,1,0:T(8,128)(2,1)S(1)}, bf16[2,2,384,384]{3,2,1,0:T(8,128)(2,1)}, u32[]{:S(2)}) %copy-start) | copy-done | bytes 1179672
  1.4 2.6 %collective-permute-start.1 = (bf16[2,2,256,256]{3,2,1,0:T(8,128)(2,1)S(1)}, bf16[2,2,256,256]{3,2,1,0:T(8,128)(2,1)S(1)}, u32[]{:S(2)}, u32[]{:S(2)}) collective-permute-start(bf16[2,2,256,256]{3,2,1,0:T(8,128)(2,1)S(1)} %get-tuple-element.18), channel_id=1, source_target_pairs={{2,0},{5,1},{6,4},{7,3},{9,5},{10,8},{11,7},{13,9},{14,12},{15,11}... | collective-permute-start | bytes 1572872 | tf_op jit(solution)/shard_map/ppermute | solution.py:339
  4.0 1.3 %collective-permute-start = (bf16[2,2,128,256]{3,2,1,0:T(8,128)(2,1)S(1)}, bf16[2,2,128,256]{3,2,1,0:T(8,128)(2,1)S(1)}, u32[]{:S(2)}, u32[]{:S(2)}) collective-permute-start(bf16[2,2,128,256]{3,2,1,0:T(8,128)(2,1)S(1)} %get-tuple-element.17), channel_id=1, source_target_pairs={{2,0},{5,1},{6,4},{7,3},{9,5},{10,8},{11,7},{13,9},{14,12},{15,11}... | collective-permute-start | bytes 786440 | tf_op jit(solution)/shard_map/ppermute | solution.py:339
  5.3 8.1 %collective-permute-done.one = bf16[2,2,128,256]{3,2,1,0:T(8,128)(2,1)S(1)} collective-permute-done((bf16[2,2,128,256]{3,2,1,0:T(8,128)(2,1)S(1)}, bf16[2,2,128,256]{3,2,1,0:T(8,128)(2,1)S(1)}, u32[]{:S(2)}, u32[]{:S(2)}) %collective-permute-start) | collective-permute-done | bytes 262176 | tf_op jit(solution)/shard_map/ppermute | solution.py:339
  13.4 1.9 %collective-permute-start.2 = (bf16[2,2,128,256]{3,2,1,0:T(8,128)(2,1)S(1)}, bf16[2,2,128,256]{3,2,1,0:T(8,128)(2,1)S(1)}, u32[]{:S(2)}, u32[]{:S(2)}) collective-permute-start(bf16[2,2,128,256]{3,2,1,0:T(8,128)(2,1)S(1)} %collective-permute-done.one), channel_id=1, source_target_pairs={{3,1},{4,0},{6,2},{7,5},{8,4},{10,6},{11,9},{12,8},{14,10},{15,13}... | collective-permute-start | bytes 786440 | tf_op jit(solution)/shard_map/ppermute | solution.py:339
  15.5 2.7 %shard_map.73 = (bf16[2,2,640,256]{3,2,1,0:T(8,128)(2,1)S(1)}, bf16[2,2,256,640]{3,2,1,0:T(8,128)(2,1)S(1)}, bf16[2,2,256,256]{3,2,1,0:T(8,128)(2,1)S(1)}) custom-call(s32[4]{0:T(128)S(1)} %reshape.6.offs, bf16[2,2,384,384]{3,2,1,0:T(8,128)(2,1)S(1)} %copy-done.1), custom_call_target="tpu_custom_call" | custom-call | tf_op jit(solution)/shard_map/pallas_call | solution.py:314
  18.2 1.4 %shard_map.75.held = bf16[2,2,2,256,256]{4,3,2,1,0:T(8,128)(2,1)S(1)} custom-call(bf16[2,2,640,256]{3,2,1,0:T(8,128)(2,1)S(1)} %get-tuple-element.14.tall, bf16[2,2,256,640]{3,2,1,0:T(8,128)(2,1)S(1)} %get-tuple-element.15.wide, bf16[2,2,256,256]{3,2,1,0:T(8,128)(2,1)S(1)} %get-tuple-element.16.held, bf16[2,2,128,256]{3,2,1,0:T(8,128)(2,1)S(1)} %collective-permute-done.one, ...), custom_call_target="tpu_custom_call" | custom-call | tf_op jit(solution)/shard_map/pallas_call | solution.py:314
  19.6 2.1 %collective-permute-done.2.three = bf16[2,2,128,256]{3,2,1,0:T(8,128)(2,1)S(1)} collective-permute-done((bf16[2,2,128,256]{3,2,1,0:T(8,128)(2,1)S(1)}, bf16[2,2,128,256]{3,2,1,0:T(8,128)(2,1)S(1)}, u32[]{:S(2)}, u32[]{:S(2)}) %collective-permute-start.2) | collective-permute-done | bytes 262176 | tf_op jit(solution)/shard_map/ppermute | solution.py:339
  21.7 1.1 %shard_map.76 = (bf16[2,2,256,256]{3,2,1,0:T(8,128)(2,1)S(1)}, bf16[2,2,256,256]{3,2,1,0:T(8,128)(2,1)S(1)}) custom-call(bf16[2,2,640,256]{3,2,1,0:T(8,128)(2,1)S(1)} %get-tuple-element.14.tall, bf16[2,2,256,640]{3,2,1,0:T(8,128)(2,1)S(1)} %get-tuple-element.15.wide, bf16[2,2,2,256,256]{4,3,2,1,0:T(8,128)(2,1)S(1)} %shard_map.75.held, ...), custom_call_target="tpu_custom_call" | custom-call | tf_op jit(solution)/shard_map/pallas_call | solution.py:314
  22.8 0.5 collective-permute-start.3
  24.1 1.2 %collective-permute-done.4.probe_b = bf16[2,256,256]{2,1,0:T(8,128)(2,1)S(1)} collective-permute-done((bf16[2,256,256]{2,1,0:T(8,128)(2,1)S(1)}, bf16[2,256,256]{2,1,0:T(8,128)(2,1)S(1)}, u32[]{:S(2)}, u32[]{:S(2)}) %collective-permute-start.4) | collective-permute-done | bytes 262176 | tf_op jit(solution)/shard_map/ppermute | solution.py:342
  25.3 4.0 %shard_map.77.kept = bf16[2,2,256,256]{3,2,1,0:T(8,128)(2,1)S(1)} custom-call(s32[1]{0:T(128)} %bitcast.3.counts, bf16[2,2,256,256]{3,2,1,0:T(8,128)(2,1)S(1)} %get-tuple-element.19.kept, bf16[2,2,256,256]{3,2,1,0:T(8,128)(2,1)S(1)} %collective-permute-done.3.got, bf16[2,256,256]{2,1,0:T(8,128)(2,1)S(1)} %bitcast.5, ...), custom_call_target="tpu_custom_call" | custom-call | tf_op jit(solution)/shard_map/pallas_call | solution.py:314
  29.3 0.4 collective-permute-start.5
  29.7 1.5 %collective-permute-done.5.got = bf16[2,2,256,256]{3,2,1,0:T(8,128)(2,1)S(1)} collective-permute-done((bf16[2,2,256,256]{3,2,1,0:T(8,128)(2,1)S(1)}, bf16[2,2,256,256]{3,2,1,0:T(8,128)(2,1)S(1)}, u32[]{:S(2)}, u32[]{:S(2)}) %collective-permute-start.5) | collective-permute-done | bytes 524320 | tf_op jit(solution)/shard_map/ppermute | solution.py:342
  31.3 1.1 %shard_map.79 = (bf16[2,2,256,256]{3,2,1,0:T(8,128)(2,1)S(1)}, f32[2,2,128,256]{3,2,1,0:T(8,128)S(1)}) custom-call(bf16[2,2,640,256]{3,2,1,0:T(8,128)(2,1)S(1)} %get-tuple-element.14.tall, bf16[2,2,256,640]{3,2,1,0:T(8,128)(2,1)S(1)} %get-tuple-element.15.wide, bf16[2,2,256,256]{3,2,1,0:T(8,128)(2,1)S(1)} %shard_map.77.kept, ...), custom_call_target="tpu_custom_call" | custom-call | tf_op jit(solution)/shard_map/pallas_call | solution.py:314
  32.4 1.3 %collective-permute-start.6 = (bf16[2,2,256,256]{3,2,1,0:T(8,128)(2,1)S(1)}, bf16[2,2,256,256]{3,2,1,0:T(8,128)(2,1)S(1)}, u32[]{:S(2)}, u32[]{:S(2)}) collective-permute-start(bf16[2,2,256,256]{3,2,1,0:T(8,128)(2,1)S(1)} %get-tuple-element.21), channel_id=1, source_target_pairs={{0,2},{1,5},{3,7},{4,6},{5,9},{7,11},{8,10},{9,13},{11,15},{12,14}... | collective-permute-start | bytes 1572872 | tf_op jit(solution)/shard_map/ppermute | solution.py:339
  33.7 0.6 %shard_map.80 = bf16[2,2,128,256]{3,2,1,0:T(8,128)(2,1)S(1)} custom-call(bf16[2,2,640,256]{3,2,1,0:T(8,128)(2,1)S(1)} %get-tuple-element.14.tall, bf16[2,2,256,640]{3,2,1,0:T(8,128)(2,1)S(1)} %get-tuple-element.15.wide, bf16[2,2,256,256]{3,2,1,0:T(8,128)(2,1)S(1)} %shard_map.77.kept, bf16[2,2,256,256]{3,2,1,0:T(8,128)(2,1)S(1)} %collective-permute-done.5.got), custom_call_target="tpu_custom_call" | custom-call | tf_op jit(solution)/shard_map/pallas_call | solution.py:314
  34.3 1.3 %collective-permute-start.8 = (bf16[2,2,128,256]{3,2,1,0:T(8,128)(2,1)S(1)}, bf16[2,2,128,256]{3,2,1,0:T(8,128)(2,1)S(1)}, u32[]{:S(2)}, u32[]{:S(2)}) collective-permute-start(bf16[2,2,128,256]{3,2,1,0:T(8,128)(2,1)S(1)} %shard_map.80), channel_id=1, source_target_pairs={{0,2},{1,5},{3,7},{4,6},{5,9},{7,11},{8,10},{9,13},{11,15},{12,14}... | collective-permute-start | bytes 786440 | tf_op jit(solution)/shard_map/ppermute | solution.py:339
  35.6 10.7 %collective-permute-done.8.got = bf16[2,2,128,256]{3,2,1,0:T(8,128)(2,1)S(1)} collective-permute-done((bf16[2,2,128,256]{3,2,1,0:T(8,128)(2,1)S(1)}, bf16[2,2,128,256]{3,2,1,0:T(8,128)(2,1)S(1)}, u32[]{:S(2)}, u32[]{:S(2)}) %collective-permute-start.8) | collective-permute-done | bytes 262176 | tf_op jit(solution)/shard_map/ppermute | solution.py:339
  46.3 3.5 %collective-permute-start.9 = (bf16[2,2,128,256]{3,2,1,0:T(8,128)(2,1)S(1)}, bf16[2,2,128,256]{3,2,1,0:T(8,128)(2,1)S(1)}, u32[]{:S(2)}, u32[]{:S(2)}) collective-permute-start(bf16[2,2,128,256]{3,2,1,0:T(8,128)(2,1)S(1)} %shard_map.81), channel_id=1, source_target_pairs={{0,4},{1,3},{2,6},{4,8},{5,7},{6,10},{8,12},{9,11},{10,14},{13,15}... | collective-permute-start | bytes 786440 | tf_op jit(solution)/shard_map/ppermute | solution.py:339
  49.9 4.7 %collective-permute-done.9.three_mine = bf16[2,2,128,256]{3,2,1,0:T(8,128)(2,1)S(1)} collective-permute-done((bf16[2,2,128,256]{3,2,1,0:T(8,128)(2,1)S(1)}, bf16[2,2,128,256]{3,2,1,0:T(8,128)(2,1)S(1)}, u32[]{:S(2)}, u32[]{:S(2)}) %collective-permute-start.9) | collective-permute-done | bytes 262176 | tf_op jit(solution)/shard_map/ppermute | solution.py:339
  54.6 0.9 %shard_map.78.own = f32[2,384,384]{2,1,0:T(8,128)S(1)} custom-call(bf16[2,2,640,256]{3,2,1,0:T(8,128)(2,1)S(1)} %get-tuple-element.14.tall, bf16[2,2,256,640]{3,2,1,0:T(8,128)(2,1)S(1)} %get-tuple-element.15.wide, bf16[2,2,256,256]{3,2,1,0:T(8,128)(2,1)S(1)} %shard_map.77.kept, bf16[2,2,256,256]{3,2,1,0:T(8,128)(2,1)S(1)} %collective-permute-done.5.got), custom_call_target="tpu_custom_call" | custom-call | tf_op jit(solution)/shard_map/pallas_call | solution.py:314
  55.4 0.7 %collective-permute-done.10.three_other = bf16[2,2,128,256]{3,2,1,0:T(8,128)(2,1)S(1)} collective-permute-done((bf16[2,2,128,256]{3,2,1,0:T(8,128)(2,1)S(1)}, bf16[2,2,128,256]{3,2,1,0:T(8,128)(2,1)S(1)}, u32[]{:S(2)}, u32[]{:S(2)}) %collective-permute-start.10) | collective-permute-done | bytes 262176 | tf_op jit(solution)/shard_map/ppermute | solution.py:342
  56.1 1.1 %shard_map.82 = f32[1,2,384,384]{3,2,1,0:T(8,128)} custom-call(f32[2,384,384]{2,1,0:T(8,128)S(1)} %shard_map.78.own, bf16[2,2,256,256]{3,2,1,0:T(8,128)(2,1)S(1)} %collective-permute-done.6.two_mine, bf16[2,2,256,256]{3,2,1,0:T(8,128)(2,1)S(1)} %collective-permute-done.7.two_other, bf16[2,2,128,256]{3,2,1,0:T(8,128)(2,1)S(1)} %collective-permute-done.9.three_mine, ...), custom_call_target="tpu_custom_call" | custom-call | tf_op jit(solution)/shard_map/pallas_call | solution.py:314
  (23 shorter events, 0.4 us)
Async XLA Ops:
  0.0 1.3 %copy-start = (bf16[2,2,384,384]{3,2,1,0:T(8,128)(2,1)S(1)}, bf16[2,2,384,384]{3,2,1,0:T(8,128)(2,1)}, u32[]{:S(2)}) copy-start(bf16[2,2,384,384]{3,2,1,0:T(8,128)(2,1)} %objects.3) | copy-start | bytes 3538948
  1.3 14.1 %copy-start.6 = (s32[1,1,2,2]{3,2,1,0:T(2,128)S(1)}, s32[1,1,2,2]{3,2,1,0:T(2,128)}, u32[]{:S(2)}) copy-start(s32[1,1,2,2]{3,2,1,0:T(2,128)} %param.11) | copy-start | bytes 52
  1.3 14.2 %copy-start.1 = (bf16[2,2,384,384]{3,2,1,0:T(8,128)(2,1)S(1)}, bf16[2,2,384,384]{3,2,1,0:T(8,128)(2,1)}, u32[]{:S(2)}) copy-start(bf16[2,2,384,384]{3,2,1,0:T(8,128)(2,1)} %objects.3) | copy-start | bytes 3538948
  1.4 16.8 %collective-permute-start.1 = (bf16[2,2,256,256]{3,2,1,0:T(8,128)(2,1)S(1)}, bf16[2,2,256,256]{3,2,1,0:T(8,128)(2,1)S(1)}, u32[]{:S(2)}, u32[]{:S(2)}) collective-permute-start(bf16[2,2,256,256]{3,2,1,0:T(8,128)(2,1)S(1)} %get-tuple-element.18), channel_id=1, source_target_pairs={{2,0},{5,1},{6,4},{7,3},{9,5},{10,8},{11,7},{13,9},{14,12},{15,11}... | collective-permute-start | bytes 1572872 | tf_op jit(solution)/shard_map/ppermute | solution.py:339
  4.0 9.5 %collective-permute-start = (bf16[2,2,128,256]{3,2,1,0:T(8,128)(2,1)S(1)}, bf16[2,2,128,256]{3,2,1,0:T(8,128)(2,1)S(1)}, u32[]{:S(2)}, u32[]{:S(2)}) collective-permute-start(bf16[2,2,128,256]{3,2,1,0:T(8,128)(2,1)S(1)} %get-tuple-element.17), channel_id=1, source_target_pairs={{2,0},{5,1},{6,4},{7,3},{9,5},{10,8},{11,7},{13,9},{14,12},{15,11}... | collective-permute-start | bytes 786440 | tf_op jit(solution)/shard_map/ppermute | solution.py:339
  13.4 8.3 %collective-permute-start.2 = (bf16[2,2,128,256]{3,2,1,0:T(8,128)(2,1)S(1)}, bf16[2,2,128,256]{3,2,1,0:T(8,128)(2,1)S(1)}, u32[]{:S(2)}, u32[]{:S(2)}) collective-permute-start(bf16[2,2,128,256]{3,2,1,0:T(8,128)(2,1)S(1)} %collective-permute-done.one), channel_id=1, source_target_pairs={{3,1},{4,0},{6,2},{7,5},{8,4},{10,6},{11,9},{12,8},{14,10},{15,13}... | collective-permute-start | bytes 786440 | tf_op jit(solution)/shard_map/ppermute | solution.py:339
  19.6 3.7 %copy-start.3 = (bf16[1,2,256,256]{3,2,1,0:T(8,128)(2,1)S(1)}, bf16[1,2,256,256]{3,2,1,0:T(8,128)(2,1)}, u32[]{:S(2)}) copy-start(bf16[1,2,256,256]{3,2,1,0:T(8,128)(2,1)} %param.8) | copy-start | bytes 786436
  19.6 5.6 %copy-start.2 = (bf16[6,256,256]{2,1,0:T(8,128)(2,1)S(1)}, bf16[6,256,256]{2,1,0:T(8,128)(2,1)}, u32[]{:S(2)}) copy-start(bf16[6,256,256]{2,1,0:T(8,128)(2,1)} %constant.7.tables) | copy-start | bytes 2359300
  19.6 5.6 %copy-start.4 = (f32[256,256]{1,0:T(8,128)S(1)}, f32[256,256]{1,0:T(8,128)}, u32[]{:S(2)}) copy-start(f32[256,256]{1,0:T(8,128)} %weights.1) | copy-start | bytes 786436
  19.6 5.6 %copy-start.5 = (bf16[1,1,2,256,256]{4,3,2,1,0:T(8,128)(2,1)S(1)}, bf16[1,1,2,256,256]{4,3,2,1,0:T(8,128)(2,1)}, u32[]{:S(2)}) copy-start(bf16[1,1,2,256,256]{4,3,2,1,0:T(8,128)(2,1)} %param.12) | copy-start | bytes 786436
  22.8 2.4 %collective-permute-start.3 = (bf16[2,2,256,256]{3,2,1,0:T(8,128)(2,1)S(1)}, bf16[2,2,256,256]{3,2,1,0:T(8,128)(2,1)S(1)}, u32[]{:S(2)}, u32[]{:S(2)}) collective-permute-start(bf16[2,2,256,256]{3,2,1,0:T(8,128)(2,1)S(1)} %get-tuple-element.20), channel_id=1, source_target_pairs={{0,1},{1,0},{2,3},{3,2},{4,5},{5,4},{6,7},{7,6},{8,9},{9,8},{10,11... | collective-permute-start | bytes 1572872 | tf_op jit(solution)/shard_map/ppermute | solution.py:342
  23.3 1.9 %collective-permute-start.4 = (bf16[2,256,256]{2,1,0:T(8,128)(2,1)S(1)}, bf16[2,256,256]{2,1,0:T(8,128)(2,1)S(1)}, u32[]{:S(2)}, u32[]{:S(2)}) collective-permute-start(bf16[2,256,256]{2,1,0:T(8,128)(2,1)S(1)} %bitcast.4), channel_id=1, source_target_pairs={{0,1},{1,0},{2,3},{3,2},{4,5},{5,4},{6,7},{7,6},{8,9},{9,8},{10,11... | collective-permute-start | bytes 786440 | tf_op jit(solution)/shard_map/ppermute | solution.py:342
  29.3 2.0 %collective-permute-start.5 = (bf16[2,2,256,256]{3,2,1,0:T(8,128)(2,1)S(1)}, bf16[2,2,256,256]{3,2,1,0:T(8,128)(2,1)S(1)}, u32[]{:S(2)}, u32[]{:S(2)}) collective-permute-start(bf16[2,2,256,256]{3,2,1,0:T(8,128)(2,1)S(1)} %shard_map.77.kept), channel_id=1, source_target_pairs={{0,1},{1,0},{2,3},{3,2},{4,5},{5,4},{6,7},{7,6},{8,9},{9,8},{10,11... | collective-permute-start | bytes 1572872 | tf_op jit(solution)/shard_map/ppermute | solution.py:342
  32.4 17.4 %collective-permute-start.6 = (bf16[2,2,256,256]{3,2,1,0:T(8,128)(2,1)S(1)}, bf16[2,2,256,256]{3,2,1,0:T(8,128)(2,1)S(1)}, u32[]{:S(2)}, u32[]{:S(2)}) collective-permute-start(bf16[2,2,256,256]{3,2,1,0:T(8,128)(2,1)S(1)} %get-tuple-element.21), channel_id=1, source_target_pairs={{0,2},{1,5},{3,7},{4,6},{5,9},{7,11},{8,10},{9,13},{11,15},{12,14}... | collective-permute-start | bytes 1572872 | tf_op jit(solution)/shard_map/ppermute | solution.py:339
  34.3 12.0 %collective-permute-start.8 = (bf16[2,2,128,256]{3,2,1,0:T(8,128)(2,1)S(1)}, bf16[2,2,128,256]{3,2,1,0:T(8,128)(2,1)S(1)}, u32[]{:S(2)}, u32[]{:S(2)}) collective-permute-start(bf16[2,2,128,256]{3,2,1,0:T(8,128)(2,1)S(1)} %shard_map.80), channel_id=1, source_target_pairs={{0,2},{1,5},{3,7},{4,6},{5,9},{7,11},{8,10},{9,13},{11,15},{12,14}... | collective-permute-start | bytes 786440 | tf_op jit(solution)/shard_map/ppermute | solution.py:339
  46.3 8.3 %collective-permute-start.9 = (bf16[2,2,128,256]{3,2,1,0:T(8,128)(2,1)S(1)}, bf16[2,2,128,256]{3,2,1,0:T(8,128)(2,1)S(1)}, u32[]{:S(2)}, u32[]{:S(2)}) collective-permute-start(bf16[2,2,128,256]{3,2,1,0:T(8,128)(2,1)S(1)} %shard_map.81), channel_id=1, source_target_pairs={{0,4},{1,3},{2,6},{4,8},{5,7},{6,10},{8,12},{9,11},{10,14},{13,15}... | collective-permute-start | bytes 786440 | tf_op jit(solution)/shard_map/ppermute | solution.py:339
  49.8 6.3 %collective-permute-start.7 = (bf16[2,2,256,256]{3,2,1,0:T(8,128)(2,1)S(1)}, bf16[2,2,256,256]{3,2,1,0:T(8,128)(2,1)S(1)}, u32[]{:S(2)}, u32[]{:S(2)}) collective-permute-start(bf16[2,2,256,256]{3,2,1,0:T(8,128)(2,1)S(1)} %collective-permute-done.6.two_mine), channel_id=1, source_target_pairs={{0,1},{1,0},{2,3},{3,2},{4,5},{5,4},{6,7},{7,6},{8,9},{9,8},{10,11... | collective-permute-start | bytes 1572872 | tf_op jit(solution)/shard_map/ppermute | solution.py:342
  54.6 1.5 %collective-permute-start.10 = (bf16[2,2,128,256]{3,2,1,0:T(8,128)(2,1)S(1)}, bf16[2,2,128,256]{3,2,1,0:T(8,128)(2,1)S(1)}, u32[]{:S(2)}, u32[]{:S(2)}) collective-permute-start(bf16[2,2,128,256]{3,2,1,0:T(8,128)(2,1)S(1)} %collective-permute-done.9.three_mine), channel_id=1, source_target_pairs={{0,1},{1,0},{2,3},{3,2},{4,5},{5,4},{6,7},{7,6},{8,9},{9,8},{10,11... | collective-permute-start | bytes 786440 | tf_op jit(solution)/shard_map/ppermute | solution.py:342

commit v3 on v1

v3 whole, which is shorter than its diff:
```python
import functools

import jax
import jax.numpy as jnp
import numpy as np
from jax import lax
from jax.experimental import pallas as pl
from jax.experimental.pallas import tpu as pltpu
from jax.sharding import PartitionSpec as P


fresnel = 0.5
VMEM = pl.BlockSpec(memory_space=pltpu.VMEM)
HBM = pl.BlockSpec(memory_space=pltpu.HBM)
SMEM = pl.BlockSpec(memory_space=pltpu.SMEM)
PARAMS = pltpu.CompilerParams(vmem_limit_bytes=20 * 2**20)


def host_tables(extent):
    counter = np.arange(extent)
    angles = 2.0 * np.pi / extent * (counter[:, None] * counter[None, :] % extent)
    forward = (np.cos(angles) - 1j * np.sin(angles)) / np.sqrt(extent)
    signed = (counter + extent // 2) % extent - extent // 2
    chirp = np.exp(-1j * np.pi * fresnel / extent * signed * signed)
    carry = (np.conj(forward) * chirp[None, :]) @ forward
    parts = [carry.real, carry.imag, -carry.imag, forward.real, forward.imag, -forward.imag]
    return jnp.asarray(np.stack(parts).astype(np.float32)).astype(jnp.bfloat16)


def dot(left, right):
    return jnp.dot(left, right, preferred_element_type=jnp.float32)


def one_hot(shape, row_sign, offset):
    row = lax.broadcasted_iota(jnp.int32, shape, 0)
    col = lax.broadcasted_iota(jnp.int32, shape, 1)
    return jnp.where((row - col) * row_sign == offset, 1.0, 0.0).astype(jnp.bfloat16)


def strip_moves(tile, win):
    half, rest = win // 2, tile - win
    return (
        ((half, win), ((0, 0, half, win, 0, 0),)),
        ((half, win), ((0, 0, half, win, half, 0),)),
        (
            (win, win),
            (
                (0, 0, half, win, half, 0),
                (half, 0, half, rest, 0, win),
                (half, rest, half, rest, half, win),
            ),
        ),
        ((win, win), ((0, 0, half, win, 0, 0), (half, 0, rest, win, win, 0))),
    )


def strips_kernel(strips, objects, *refs):
    me = lax.axis_index("slc")
    sems = refs[-1]
    copies = []
    for (_, moves), out in zip(strips, refs):
        for row, col, height, width, from_row, from_col in moves:
            copies.append(
                pltpu.make_async_copy(
                    objects.at[me, :, pl.ds(from_row, height), pl.ds(from_col, width)],
                    out.at[:, pl.ds(row, height), pl.ds(col, width)],
                    sems.at[len(copies)],
                )
            )
    for copy in copies:
        copy.start()
    for copy in copies:
        copy.wait()


def half_of(value):
    return value.astype(jnp.bfloat16)


def prepare_kernel(offs, objects, tall, wide, held):
    me = lax.axis_index("slc")
    tile = objects.shape[2]
    ext, win = tall.shape[2:]
    for n, slot in enumerate((me, 1 - me)):
        for dim in range(2):
            offset = offs[2 * slot + dim]
            tall[n, dim] = one_hot((ext, win), 1, offset)
            wide[n, dim] = one_hot((win, ext), -1, offset)
        for part in range(2):
            upper = half_of(dot(objects[me, part], tall[n, 1, :tile]))
            held[n, part] = half_of(dot(wide[n, 0, :, :tile], upper))


def reach_kernel(tall, wide, held, x_one, x_two, z_one, z_two, out):
    half, win = x_one.shape[1:]
    tile = tall.shape[2] - win
    rest = tile - win
    for part in range(2):
        right = jnp.concatenate([x_two[part, :half], x_one[part], x_two[part, half:]], axis=0)
        near = jnp.concatenate([z_one[part], z_two[part, :half]], axis=0)
        side = jnp.concatenate([z_two[part, half:, :rest], z_two[part, half:, rest:]], axis=0)
        below = jnp.concatenate([near, side], axis=1)
        for n in range(2):
            upper = half_of(dot(right, tall[n, 1, tile:]))
            lower = half_of(dot(below, tall[n, 1, :tile]))
            window = dot(wide[n, 0, :, :tile], upper) + dot(wide[n, 0, :, tile:], lower)
            out[n, part] = half_of(held[n, part].astype(jnp.float32) + window)


def corner_kernel(tall, wide, held, x_three, z_three, keep, send):
    win = keep.shape[1]
    tile = tall.shape[2] - win
    for n, out in ((1, send), (0, keep)):
        for part in range(2):
            corner = jnp.concatenate([x_three[part], z_three[part]], axis=0)
            lower = half_of(dot(corner, tall[n, 1, tile:]))
            window = dot(wide[n, 0, :, tile:], lower)
            out[part] = half_of(held[n, part].astype(jnp.float32) + window)


def transform(real, imag, table_re, table_im, table_in):
    real = real.astype(jnp.bfloat16)
    imag = imag.astype(jnp.bfloat16)
    mid_re = (dot(table_re, real) + dot(table_in, imag)).astype(jnp.bfloat16)
    mid_im = (dot(table_re, imag) + dot(table_im, real)).astype(jnp.bfloat16)
    out_re = dot(mid_re, table_re) + dot(mid_im, table_in)
    out_im = dot(mid_re, table_im) + dot(mid_im, table_re)
    return out_re, out_im


def complex_mul(left_re, left_im, right_re, right_im):
    return (left_re * right_re - left_im * right_im, left_re * right_im + left_im * right_re)


def conj_mul(left_re, left_im, right_re, right_im):
    return (left_re * right_re + left_im * right_im, left_re * right_im - left_im * right_re)


def grad_kernel(
    counts, kept, got, probe_a, probe_b, weights, measured, tables, keep, send, prop, far
):
    me = lax.axis_index("slc")
    carry = (tables[0], tables[1], tables[2])
    carry_conj = (tables[0], tables[2], tables[1])
    fwd = (tables[3], tables[4], tables[5])
    inv = (tables[3], tables[5], tables[4])
    first_mine = me == 0

    def pick(part, flag):
        return jnp.where(flag, kept[part], got[part]).astype(jnp.float32)

    probes = (probe_a, probe_b)
    intensity = None
    for mode, probe in enumerate(probes):
        one_re, one_im = pick(0, first_mine), pick(1, first_mine)
        psi = complex_mul(
            probe[0].astype(jnp.float32), probe[1].astype(jnp.float32), one_re, one_im
        )
        prop_re, prop_im = transform(*psi, *carry)
        prop[mode, 0] = prop_re
        prop[mode, 1] = prop_im
        two_re, two_im = pick(0, ~first_mine), pick(1, ~first_mine)
        leave = complex_mul(prop_re, prop_im, two_re, two_im)
        far_re, far_im = transform(*leave, *fwd)
        far[mode, 0] = far_re
        far[mode, 1] = far_im
        square = far_re * far_re + far_im * far_im
        intensity = square if intensity is None else intensity + square
    residual = 2.0 * weights[...] * (intensity - measured[me].astype(jnp.float32))
    residual = jnp.where(me < counts[0], residual, 0.0)
    one_sum = two_sum = None
    for mode, probe in enumerate(probes):
        back_re, back_im = transform(residual * far[mode, 0], residual * far[mode, 1], *inv)
        two = conj_mul(prop[mode, 0], prop[mode, 1], back_re, back_im)
        two_re, two_im = pick(0, ~first_mine), pick(1, ~first_mine)
        inner = conj_mul(two_re, two_im, back_re, back_im)
        gpsi_re, gpsi_im = transform(*inner, *carry_conj)
        one = conj_mul(probe[0].astype(jnp.float32), probe[1].astype(jnp.float32), gpsi_re, gpsi_im)
        one_sum = one if one_sum is None else (one_sum[0] + one[0], one_sum[1] + one[1])
        two_sum = two if two_sum is None else (two_sum[0] + two[0], two_sum[1] + two[1])
    for part in range(2):
        keep[part] = jnp.where(first_mine, one_sum[part], two_sum[part]).astype(jnp.bfloat16)
        send[part] = jnp.where(first_mine, two_sum[part], one_sum[part]).astype(jnp.bfloat16)


def tip_kernel(tall, wide, kept, got, low, x_one, z_one):
    half, win = x_one.shape[1:]
    tile = tall.shape[2] - win
    for part in range(2):
        corner = None
        for n, grad in enumerate((kept, got)):
            lower = half_of(dot(tall[n, 0, tile:], grad[part]))
            low[n, part] = lower
            term = dot(lower, wide[n, 1, :, tile:])
            corner = term if corner is None else corner + term
        x_one[part] = half_of(corner[:half])
        z_one[part] = half_of(corner[half:])


def side_kernel(tall, wide, kept, got, low, up, x_add, z_add, x_two, z_two):
    half, win = x_add.shape[1:]
    tile = tall.shape[2] - win
    rest = tile - win
    for part in range(2):
        right = below = None
        for n, grad in enumerate((kept, got)):
            upper = half_of(dot(tall[n, 0, :tile], grad[part]))
            up[n, part] = upper
            far = dot(upper, wide[n, 1, :, tile:])
            near = dot(low[n, part], wide[n, 1, :, :tile])
            right = far if right is None else right + far
            below = near if below is None else below + near
        x_two[part, :half] = half_of(right[:half])
        x_two[part, half:] = half_of(right[win:])
        x_add[part] = right[half:win]
        z_add[part] = below[:half, :win]
        z_two[part, :half] = half_of(below[half:, :win])
        z_two[part, half:, :rest] = half_of(below[:half, win:])
        z_two[part, half:, rest:] = half_of(below[half:, win:])


def add_kernel(mine, got, out):
    out[...] = half_of(mine[...] + got[...].astype(jnp.float32))


def own_kernel(wide, up, own):
    tile = own.shape[1]
    for part in range(2):
        own[part] = dot(up[0, part], wide[0, 1, :, :tile]) + dot(up[1, part], wide[1, 1, :, :tile])


def join_kernel(own, x_two, x_three, z_two, z_three, out):
    half, win = x_three.shape[1:]
    rest = own.shape[1] - win
    full = jnp.float32
    for part in range(2):
        out[0, part, win:, win:] = own[part, win:, win:]
        out[0, part, win:, :win] = own[part, win:, :win] + x_two[part, half:].astype(full)
        out[0, part, :half, win:] = own[part, :half, win:] + z_two[part, half:, :rest].astype(full)
        out[0, part, half:win, win:] = own[part, half:win, win:] + z_two[
            part, half:, rest:
        ].astype(full)
        out[0, part, :half, :win] = (
            own[part, :half, :win] + x_two[part, :half].astype(full) + z_three[part].astype(full)
        )
        out[0, part, half:win, :win] = (
            own[part, half:win, :win] + x_three[part].astype(full) + z_two[part, :half].astype(full)
        )


def call(kernel, out_shape, *args, specs=None, scratch=()):
    return pl.pallas_call(
        kernel,
        out_shape=out_shape,
        in_specs=specs or [VMEM] * len(args),
        out_specs=jax.tree.map(lambda _: VMEM, out_shape),
        scratch_shapes=scratch,
        compiler_params=PARAMS,
    )(*args)


def body(rows, cols, objects, probes, weights, counts, offsets, intensities):
    tile = objects.shape[2]
    win = probes.shape[2]
    half, ext = win // 2, tile + win
    low = jnp.bfloat16

    def shift(x, down, across):
        pairs = []
        for r in range(rows):
            for c in range(cols):
                pairs.append((r * cols + c, (r + down) % rows * cols + (c + across) % cols))
        return lax.ppermute(x, ("row", "col"), pairs)

    def swap(x):
        return lax.ppermute(x, "slc", [(0, 1), (1, 0)])

    def shape(*dims, dtype=low):
        return jax.ShapeDtypeStruct(dims, dtype)

    offs = offsets.reshape(-1)
    window = shape(2, win, win)
    strips = strip_moves(tile, win)
    z_one, x_one, z_two, x_two = call(
        functools.partial(strips_kernel, strips),
        tuple(shape(2, *dims) for dims, _ in strips),
        objects,
        specs=[HBM],
        scratch=[pltpu.SemaphoreType.DMA((sum(len(moves) for _, moves in strips),))],
    )
    z_one = shift(z_one, -1, 0)
    x_one = shift(x_one, 0, -1)
    z_two = shift(z_two, -1, 0)
    x_two = shift(x_two, 0, -1)
    probe = probes[0]
    probe_other = swap(probe)
    tall, wide, held = call(
        prepare_kernel,
        (shape(2, 2, ext, win), shape(2, 2, win, ext), shape(2, 2, win, win)),
        offs,
        objects,
        specs=[SMEM, VMEM],
    )
    x_three = shift(z_one, 0, -1)
    z_three = shift(x_one, -1, 0)
    held = call(reach_kernel, shape(2, 2, win, win), tall, wide, held, x_one, x_two, z_one, z_two)
    keep, send = call(corner_kernel, (window, window), tall, wide, held, x_three, z_three)
    got = swap(send)
    keep, send = call(
        grad_kernel,
        (window, window),
        counts.reshape(-1),
        keep,
        got,
        probe,
        probe_other,
        weights,
        intensities[0, 0],
        host_tables(win),
        specs=[SMEM] + [VMEM] * 7,
        scratch=[pltpu.VMEM((2, 2, win, win), jnp.float32)] * 2,
    )
    got = swap(send)
    piece = shape(2, half, win)
    lower, x_one, z_one = call(
        tip_kernel, (shape(2, 2, win, win), piece, piece), tall, wide, keep, got
    )
    x_one = shift(x_one, 0, 1)
    z_one = shift(z_one, 1, 0)
    addend = shape(2, half, win, dtype=jnp.float32)
    upper, x_add, z_add, x_two, z_two = call(
        side_kernel,
        (shape(2, 2, tile, win), addend, addend, window, window),
        tall,
        wide,
        keep,
        got,
        lower,
    )
    x_two = shift(x_two, 0, 1)
    z_two = shift(z_two, 1, 0)
    z_three = shift(call(add_kernel, piece, z_add, x_one), 1, 0)
    x_three = shift(call(add_kernel, piece, x_add, z_one), 0, 1)
    own = call(own_kernel, shape(2, tile, tile, dtype=jnp.float32), wide, upper)
    return call(
        join_kernel, shape(1, 2, tile, tile, dtype=jnp.float32), own, x_two, x_three, z_two, z_three
    )


def staged(rows, cols, *args):
    return body(rows, cols, *args)


def solution(mesh):
    in_specs = (
        P(None, None, ("grp", "row"), "col"),
        P(("grp", "slc"), None, None, None),
        P(),
        P(("grp", "row"), "col"),
        P(("grp", "row"), "col", None, None),
        P(("grp", "row"), "col", None, None, None),
    )
    out_specs = P("slc", None, ("grp", "row"), "col")
    run = functools.partial(staged, mesh.shape["row"], mesh.shape["col"])
    return jax.shard_map(run, mesh=mesh, in_specs=in_specs, out_specs=out_specs, check_vma=False)
```

time: 61.5 us -> 49.2 us (0.80)
  the two profiles are of different devices: /device:TPU:10 before, /device:TPU:0 now
where the time goes in v3:
time: 49.2 us; the launch traced here: 49.1 us
  waiting for transfers between devices  17.8 us (36%)
  starting transfers between devices  16.8 us (34%)
  Pallas kernels  12.2 us (25%)
  local copies, waits for them, and re-layouts  1.38 us (3%)
  between operations  0.82 us (2%)
    ppermute x12, waiting for transfers between devices, shift(): return lax.ppermute(x, ('row', 'col'), pairs)  16.1 us
    ppermute x12, starting transfers between devices, shift(): return lax.ppermute(x, ('row', 'col'), pairs)  15.8 us
    pallas_call x11, Pallas kernels, call(): pl.pallas_call(kernel, out_shape=out_shape, in_specs=specs or [VMEM] * le...  12.2 us
    ppermute x3, waiting for transfers between devices, swap(): return lax.ppermute(x, 'slc', [(0, 1), (1, 0)])  1.67 us
    unnamed x14, local copies, waits for them, and re-layouts  1.3 us
    ppermute x3, starting transfers between devices, swap(): return lax.ppermute(x, 'slc', [(0, 1), (1, 0)])  1.02 us
  transfers between devices with their start and end apart: 15, of which 6 were waited for; matrix products, arithmetic and copies ran while one was open for 0% of the time, Pallas kernels for 13%

profile of v3, /device:TPU:0, one launch (start us, length us, event | category | flops | bytes accessed | tf_op | source)
XLA Modules:
  0.0 49.1 jit_solution(13564714973159567247)
XLA Ops:
  0.0 1.3 %copy-done = bf16[2,2,384,384]{3,2,1,0:T(8,128)(2,1)S(1)} copy-done((bf16[2,2,384,384]{3,2,1,0:T(8,128)(2,1)S(1)}, bf16[2,2,384,384]{3,2,1,0:T(8,128)(2,1)}, u32[]{:S(2)}) %copy-start) | copy-done | bytes 1179672
  1.4 3.0 %collective-permute-start.1 = (bf16[2,256,256]{2,1,0:T(8,128)(2,1)S(1)}, bf16[2,256,256]{2,1,0:T(8,128)(2,1)S(1)}, u32[]{:S(2)}, u32[]{:S(2)}) collective-permute-start(bf16[2,256,256]{2,1,0:T(8,128)(2,1)S(1)} %get-tuple-element.28), channel_id=1, source_target_pairs={{0,2},{2,0},{4,6},{6,4},{8,10},{10,8},{12,14},{14,12},{1,3},{3,1},... | collective-permute-start | bytes 786440 | tf_op jit(solution)/shard_map/ppermute | solution.py:273
  4.5 3.6 %collective-permute-start.3 = (bf16[2,256,256]{2,1,0:T(8,128)(2,1)S(1)}, bf16[2,256,256]{2,1,0:T(8,128)(2,1)S(1)}, u32[]{:S(2)}, u32[]{:S(2)}) collective-permute-start(bf16[2,256,256]{2,1,0:T(8,128)(2,1)S(1)} %get-tuple-element.30), channel_id=1, source_target_pairs={{0,12},{2,14},{4,0},{6,2},{8,4},{10,6},{12,8},{14,10},{1,13},{3,15... | collective-permute-start | bytes 786440 | tf_op jit(solution)/shard_map/ppermute | solution.py:273
  8.1 0.5 %collective-permute-start = (bf16[2,128,256]{2,1,0:T(8,128)(2,1)S(1)}, bf16[2,128,256]{2,1,0:T(8,128)(2,1)S(1)}, u32[]{:S(2)}, u32[]{:S(2)}) collective-permute-start(bf16[2,128,256]{2,1,0:T(8,128)(2,1)S(1)} %get-tuple-element.27), channel_id=1, source_target_pairs={{0,2},{2,0},{4,6},{6,4},{8,10},{10,8},{12,14},{14,12},{1,3},{3,1},... | collective-permute-start | bytes 393224 | tf_op jit(solution)/shard_map/ppermute | solution.py:273
  9.0 4.5 %collective-permute-done.x_one = bf16[2,128,256]{2,1,0:T(8,128)(2,1)S(1)} collective-permute-done((bf16[2,128,256]{2,1,0:T(8,128)(2,1)S(1)}, bf16[2,128,256]{2,1,0:T(8,128)(2,1)S(1)}, u32[]{:S(2)}, u32[]{:S(2)}) %collective-permute-start) | collective-permute-done | bytes 131104 | tf_op jit(solution)/shard_map/ppermute | solution.py:273
  13.6 3.9 %collective-permute-start.5 = (bf16[2,128,256]{2,1,0:T(8,128)(2,1)S(1)}, bf16[2,128,256]{2,1,0:T(8,128)(2,1)S(1)}, u32[]{:S(2)}, u32[]{:S(2)}) collective-permute-start(bf16[2,128,256]{2,1,0:T(8,128)(2,1)S(1)} %collective-permute-done.x_one), channel_id=1, source_target_pairs={{0,12},{2,14},{4,0},{6,2},{8,4},{10,6},{12,8},{14,10},{1,13},{3,15... | collective-permute-start | bytes 393224 | tf_op jit(solution)/shard_map/ppermute | solution.py:273
  17.4 1.5 %collective-permute-start.4 = (bf16[2,128,256]{2,1,0:T(8,128)(2,1)S(1)}, bf16[2,128,256]{2,1,0:T(8,128)(2,1)S(1)}, u32[]{:S(2)}, u32[]{:S(2)}) collective-permute-start(bf16[2,128,256]{2,1,0:T(8,128)(2,1)S(1)} %collective-permute-done.2.z_one), channel_id=1, source_target_pairs={{0,2},{2,0},{4,6},{6,4},{8,10},{10,8},{12,14},{14,12},{1,3},{3,1},... | collective-permute-start | bytes 393224 | tf_op jit(solution)/shard_map/ppermute | solution.py:273
  19.0 2.6 %shard_map.73 = (bf16[2,2,640,256]{3,2,1,0:T(8,128)(2,1)S(1)}, bf16[2,2,256,640]{3,2,1,0:T(8,128)(2,1)S(1)}, bf16[2,2,256,256]{3,2,1,0:T(8,128)(2,1)S(1)}) custom-call(s32[4]{0:T(128)S(1)} %reshape.6.offs, bf16[2,2,384,384]{3,2,1,0:T(8,128)(2,1)S(1)} %copy-done.1), custom_call_target="tpu_custom_call" | custom-call | tf_op jit(solution)/shard_map/pallas_call | solution.py:252
  21.7 1.5 %shard_map.75.held = bf16[2,2,256,256]{3,2,1,0:T(8,128)(2,1)S(1)} custom-call(bf16[2,2,640,256]{3,2,1,0:T(8,128)(2,1)S(1)} %get-tuple-element.25.tall, bf16[2,2,256,640]{3,2,1,0:T(8,128)(2,1)S(1)} %get-tuple-element.24.wide, bf16[2,2,256,256]{3,2,1,0:T(8,128)(2,1)S(1)} %get-tuple-element.26.held, bf16[2,128,256]{2,1,0:T(8,128)(2,1)S(1)} %collective-permute-done.x_one, ...), custom_call_target="tpu_custom_call" | custom-call | tf_op jit(solution)/shard_map/pallas_call | solution.py:252
  23.3 0.6 %shard_map.76 = (bf16[2,256,256]{2,1,0:T(8,128)(2,1)S(1)}, bf16[2,256,256]{2,1,0:T(8,128)(2,1)S(1)}) custom-call(bf16[2,2,640,256]{3,2,1,0:T(8,128)(2,1)S(1)} %get-tuple-element.25.tall, bf16[2,2,256,640]{3,2,1,0:T(8,128)(2,1)S(1)} %get-tuple-element.24.wide, bf16[2,2,256,256]{3,2,1,0:T(8,128)(2,1)S(1)} %shard_map.75.held, ...), custom_call_target="tpu_custom_call" | custom-call | tf_op jit(solution)/shard_map/pallas_call | solution.py:252
  23.9 0.6 %collective-permute-start.6 = (bf16[2,256,256]{2,1,0:T(8,128)(2,1)S(1)}, bf16[2,256,256]{2,1,0:T(8,128)(2,1)S(1)}, u32[]{:S(2)}, u32[]{:S(2)}) collective-permute-start(bf16[2,256,256]{2,1,0:T(8,128)(2,1)S(1)} %get-tuple-element.32), channel_id=1, source_target_pairs={{0,1},{1,0},{2,3},{3,2},{4,5},{5,4},{6,7},{7,6},{8,9},{9,8},{10,11... | collective-permute-start | bytes 786440 | tf_op jit(solution)/shard_map/ppermute | solution.py:276
  25.1 0.5 %collective-permute-done.6.got = bf16[2,256,256]{2,1,0:T(8,128)(2,1)S(1)} collective-permute-done((bf16[2,256,256]{2,1,0:T(8,128)(2,1)S(1)}, bf16[2,256,256]{2,1,0:T(8,128)(2,1)S(1)}, u32[]{:S(2)}, u32[]{:S(2)}) %collective-permute-start.6) | collective-permute-done | bytes 262176 | tf_op jit(solution)/shard_map/ppermute | solution.py:276
  25.6 4.1 %shard_map.77 = (bf16[2,256,256]{2,1,0:T(8,128)(2,1)S(1)}, bf16[2,256,256]{2,1,0:T(8,128)(2,1)S(1)}) custom-call(s32[1]{0:T(128)} %bitcast.3.counts, bf16[2,256,256]{2,1,0:T(8,128)(2,1)S(1)} %get-tuple-element.31.kept, bf16[2,256,256]{2,1,0:T(8,128)(2,1)S(1)} %collective-permute-done.6.got, bf16[2,256,256]{2,1,0:T(8,128)(2,1)S(1)} %bitcast.5, ...), custom_call_target="tpu_custom_call" | custom-call | tf_op jit(solution)/shard_map/pallas_call | solution.py:252
  30.1 1.2 %collective-permute-done.8.got = bf16[2,256,256]{2,1,0:T(8,128)(2,1)S(1)} collective-permute-done((bf16[2,256,256]{2,1,0:T(8,128)(2,1)S(1)}, bf16[2,256,256]{2,1,0:T(8,128)(2,1)S(1)}, u32[]{:S(2)}, u32[]{:S(2)}) %collective-permute-start.8) | collective-permute-done | bytes 262176 | tf_op jit(solution)/shard_map/ppermute | solution.py:276
  31.3 0.6 %shard_map.78 = (bf16[2,2,256,256]{3,2,1,0:T(8,128)(2,1)S(1)}, bf16[2,128,256]{2,1,0:T(8,128)(2,1)S(1)}, bf16[2,128,256]{2,1,0:T(8,128)(2,1)S(1)}) custom-call(bf16[2,2,640,256]{3,2,1,0:T(8,128)(2,1)S(1)} %get-tuple-element.25.tall, bf16[2,2,256,640]{3,2,1,0:T(8,128)(2,1)S(1)} %get-tuple-element.24.wide, bf16[2,256,256]{2,1,0:T(8,128)(2,1)S(1)} %get-tuple-element.33.kept, ...), custom_call_target="tpu_custom_call" | custom-call | tf_op jit(solution)/shard_map/pallas_call | solution.py:252
  32.0 0.6 %collective-permute-start.13 = (bf16[2,128,256]{2,1,0:T(8,128)(2,1)S(1)}, bf16[2,128,256]{2,1,0:T(8,128)(2,1)S(1)}, u32[]{:S(2)}, u32[]{:S(2)}) collective-permute-start(bf16[2,128,256]{2,1,0:T(8,128)(2,1)S(1)} %get-tuple-element.42), channel_id=1, source_target_pairs={{0,2},{2,0},{4,6},{6,4},{8,10},{10,8},{12,14},{14,12},{1,3},{3,1},... | collective-permute-start | bytes 393224 | tf_op jit(solution)/shard_map/ppermute | solution.py:273
  32.6 0.9 %shard_map.79 = (bf16[2,2,384,256]{3,2,1,0:T(8,128)(2,1)S(1)}, f32[2,128,256]{2,1,0:T(8,128)S(1)}, f32[2,128,256]{2,1,0:T(8,128)S(1)}, bf16[2,256,256]{2,1,0:T(8,128)(2,1)S(1)}, bf16[2,256,256]{2,1,0:T(8,128)(2,1)S(1)}) custom-call(bf16[2,2,640,256]{3,2,1,0:T(8,128)(2,1)S(1)} %get-tuple-element.25.tall, bf16[2,2,256,640]{3,2,1,0:T(8,128)(2,1)S(1)} %get-tuple-element.24.wide, ...), custom_call_target="tpu_custom_call" | custom-call | tf_op jit(solution)/shard_map/pallas_call | solution.py:252
  33.5 1.6 %collective-permute-start.9 = (bf16[2,256,256]{2,1,0:T(8,128)(2,1)S(1)}, bf16[2,256,256]{2,1,0:T(8,128)(2,1)S(1)}, u32[]{:S(2)}, u32[]{:S(2)}) collective-permute-start(bf16[2,256,256]{2,1,0:T(8,128)(2,1)S(1)} %get-tuple-element.37), channel_id=1, source_target_pairs={{0,2},{2,0},{4,6},{6,4},{8,10},{10,8},{12,14},{14,12},{1,3},{3,1},... | collective-permute-start | bytes 786440 | tf_op jit(solution)/shard_map/ppermute | solution.py:273
  35.1 4.7 %collective-permute-done.10.got = bf16[2,128,256]{2,1,0:T(8,128)(2,1)S(1)} collective-permute-done((bf16[2,128,256]{2,1,0:T(8,128)(2,1)S(1)}, bf16[2,128,256]{2,1,0:T(8,128)(2,1)S(1)}, u32[]{:S(2)}, u32[]{:S(2)}) %collective-permute-start.10) | collective-permute-done | bytes 131104 | tf_op jit(solution)/shard_map/ppermute | solution.py:273
  39.8 0.6 %collective-permute-start.11 = (bf16[2,128,256]{2,1,0:T(8,128)(2,1)S(1)}, bf16[2,128,256]{2,1,0:T(8,128)(2,1)S(1)}, u32[]{:S(2)}, u32[]{:S(2)}) collective-permute-start(bf16[2,128,256]{2,1,0:T(8,128)(2,1)S(1)} %shard_map.81), channel_id=1, source_target_pairs={{0,2},{2,0},{4,6},{6,4},{8,10},{10,8},{12,14},{14,12},{1,3},{3,1},... | collective-permute-start | bytes 393224 | tf_op jit(solution)/shard_map/ppermute | solution.py:273
  40.5 0.6 %shard_map.80.own = f32[2,384,384]{2,1,0:T(8,128)S(1)} custom-call(bf16[2,2,256,640]{3,2,1,0:T(8,128)(2,1)S(1)} %get-tuple-element.24.wide, bf16[2,2,384,256]{3,2,1,0:T(8,128)(2,1)S(1)} %get-tuple-element.36.up), custom_call_target="tpu_custom_call" | custom-call | tf_op jit(solution)/shard_map/pallas_call | solution.py:252
  41.1 5.2 %collective-permute-done.11.x_three = bf16[2,128,256]{2,1,0:T(8,128)(2,1)S(1)} collective-permute-done((bf16[2,128,256]{2,1,0:T(8,128)(2,1)S(1)}, bf16[2,128,256]{2,1,0:T(8,128)(2,1)S(1)}, u32[]{:S(2)}, u32[]{:S(2)}) %collective-permute-start.11) | collective-permute-done | bytes 131104 | tf_op jit(solution)/shard_map/ppermute | solution.py:273
  46.2 1.7 %collective-permute-done.14.z_three = bf16[2,128,256]{2,1,0:T(8,128)(2,1)S(1)} collective-permute-done((bf16[2,128,256]{2,1,0:T(8,128)(2,1)S(1)}, bf16[2,128,256]{2,1,0:T(8,128)(2,1)S(1)}, u32[]{:S(2)}, u32[]{:S(2)}) %collective-permute-start.14) | collective-permute-done | bytes 131104 | tf_op jit(solution)/shard_map/ppermute | solution.py:273
  48.0 1.1 %shard_map.83 = f32[1,2,384,384]{3,2,1,0:T(8,128)} custom-call(f32[2,384,384]{2,1,0:T(8,128)S(1)} %shard_map.80.own, bf16[2,256,256]{2,1,0:T(8,128)(2,1)S(1)} %collective-permute-done.9.x_two, bf16[2,128,256]{2,1,0:T(8,128)(2,1)S(1)} %collective-permute-done.11.x_three, bf16[2,256,256]{2,1,0:T(8,128)(2,1)S(1)} %collective-permute-done.12.z_two, ...), custom_call_target="tpu_custom_call" | custom-call | tf_op jit(solution)/shard_map/pallas_call | solution.py:252
  (32 shorter events, 1.4 us)
Async XLA Ops:
  0.0 1.3 %copy-start = (bf16[2,2,384,384]{3,2,1,0:T(8,128)(2,1)S(1)}, bf16[2,2,384,384]{3,2,1,0:T(8,128)(2,1)}, u32[]{:S(2)}) copy-start(bf16[2,2,384,384]{3,2,1,0:T(8,128)(2,1)} %objects.3) | copy-start | bytes 3538948
  1.3 17.7 %copy-start.6 = (s32[1,1,2,2]{3,2,1,0:T(2,128)S(1)}, s32[1,1,2,2]{3,2,1,0:T(2,128)}, u32[]{:S(2)}) copy-start(s32[1,1,2,2]{3,2,1,0:T(2,128)} %param.11) | copy-start | bytes 52
  1.3 17.7 %copy-start.1 = (bf16[2,2,384,384]{3,2,1,0:T(8,128)(2,1)S(1)}, bf16[2,2,384,384]{3,2,1,0:T(8,128)(2,1)}, u32[]{:S(2)}) copy-start(bf16[2,2,384,384]{3,2,1,0:T(8,128)(2,1)} %objects.3) | copy-start | bytes 3538948
  1.4 20.2 %collective-permute-start.1 = (bf16[2,256,256]{2,1,0:T(8,128)(2,1)S(1)}, bf16[2,256,256]{2,1,0:T(8,128)(2,1)S(1)}, u32[]{:S(2)}, u32[]{:S(2)}) collective-permute-start(bf16[2,256,256]{2,1,0:T(8,128)(2,1)S(1)} %get-tuple-element.28), channel_id=1, source_target_pairs={{0,2},{2,0},{4,6},{6,4},{8,10},{10,8},{12,14},{14,12},{1,3},{3,1},... | collective-permute-start | bytes 786440 | tf_op jit(solution)/shard_map/ppermute | solution.py:273
  4.5 17.2 %collective-permute-start.3 = (bf16[2,256,256]{2,1,0:T(8,128)(2,1)S(1)}, bf16[2,256,256]{2,1,0:T(8,128)(2,1)S(1)}, u32[]{:S(2)}, u32[]{:S(2)}) collective-permute-start(bf16[2,256,256]{2,1,0:T(8,128)(2,1)S(1)} %get-tuple-element.30), channel_id=1, source_target_pairs={{0,12},{2,14},{4,0},{6,2},{8,4},{10,6},{12,8},{14,10},{1,13},{3,15... | collective-permute-start | bytes 786440 | tf_op jit(solution)/shard_map/ppermute | solution.py:273
  8.1 5.5 %collective-permute-start = (bf16[2,128,256]{2,1,0:T(8,128)(2,1)S(1)}, bf16[2,128,256]{2,1,0:T(8,128)(2,1)S(1)}, u32[]{:S(2)}, u32[]{:S(2)}) collective-permute-start(bf16[2,128,256]{2,1,0:T(8,128)(2,1)S(1)} %get-tuple-element.27), channel_id=1, source_target_pairs={{0,2},{2,0},{4,6},{6,4},{8,10},{10,8},{12,14},{14,12},{1,3},{3,1},... | collective-permute-start | bytes 393224 | tf_op jit(solution)/shard_map/ppermute | solution.py:273
  8.6 8.8 %collective-permute-start.2 = (bf16[2,128,256]{2,1,0:T(8,128)(2,1)S(1)}, bf16[2,128,256]{2,1,0:T(8,128)(2,1)S(1)}, u32[]{:S(2)}, u32[]{:S(2)}) collective-permute-start(bf16[2,128,256]{2,1,0:T(8,128)(2,1)S(1)} %get-tuple-element.29), channel_id=1, source_target_pairs={{0,12},{2,14},{4,0},{6,2},{8,4},{10,6},{12,8},{14,10},{1,13},{3,15... | collective-permute-start | bytes 393224 | tf_op jit(solution)/shard_map/ppermute | solution.py:273
  13.6 9.7 %collective-permute-start.5 = (bf16[2,128,256]{2,1,0:T(8,128)(2,1)S(1)}, bf16[2,128,256]{2,1,0:T(8,128)(2,1)S(1)}, u32[]{:S(2)}, u32[]{:S(2)}) collective-permute-start(bf16[2,128,256]{2,1,0:T(8,128)(2,1)S(1)} %collective-permute-done.x_one), channel_id=1, source_target_pairs={{0,12},{2,14},{4,0},{6,2},{8,4},{10,6},{12,8},{14,10},{1,13},{3,15... | collective-permute-start | bytes 393224 | tf_op jit(solution)/shard_map/ppermute | solution.py:273
  17.4 5.8 %collective-permute-start.4 = (bf16[2,128,256]{2,1,0:T(8,128)(2,1)S(1)}, bf16[2,128,256]{2,1,0:T(8,128)(2,1)S(1)}, u32[]{:S(2)}, u32[]{:S(2)}) collective-permute-start(bf16[2,128,256]{2,1,0:T(8,128)(2,1)S(1)} %collective-permute-done.2.z_one), channel_id=1, source_target_pairs={{0,2},{2,0},{4,6},{6,4},{8,10},{10,8},{12,14},{14,12},{1,3},{3,1},... | collective-permute-start | bytes 393224 | tf_op jit(solution)/shard_map/ppermute | solution.py:273
  18.9 6.2 %collective-permute-start.7 = (bf16[2,256,256]{2,1,0:T(8,128)(2,1)}, bf16[2,256,256]{2,1,0:T(8,128)(2,1)S(1)}, u32[]{:S(2)}, u32[]{:S(2)}) collective-permute-start(bf16[2,256,256]{2,1,0:T(8,128)(2,1)} %bitcast.4), channel_id=1, source_target_pairs={{0,1},{1,0},{2,3},{3,2},{4,5},{5,4},{6,7},{7,6},{8,9},{9,8},{10,11... | collective-permute-start | bytes 786440 | tf_op jit(solution)/shard_map/ppermute | solution.py:276
  23.2 2.4 %copy-start.2 = (bf16[6,256,256]{2,1,0:T(8,128)(2,1)S(1)}, bf16[6,256,256]{2,1,0:T(8,128)(2,1)}, u32[]{:S(2)}) copy-start(bf16[6,256,256]{2,1,0:T(8,128)(2,1)} %constant.7.tables) | copy-start | bytes 2359300
  23.2 2.4 %copy-start.3 = (bf16[1,2,256,256]{3,2,1,0:T(8,128)(2,1)S(1)}, bf16[1,2,256,256]{3,2,1,0:T(8,128)(2,1)}, u32[]{:S(2)}) copy-start(bf16[1,2,256,256]{3,2,1,0:T(8,128)(2,1)} %param.8) | copy-start | bytes 786436
  23.2 2.4 %copy-start.4 = (f32[256,256]{1,0:T(8,128)S(1)}, f32[256,256]{1,0:T(8,128)}, u32[]{:S(2)}) copy-start(f32[256,256]{1,0:T(8,128)} %weights.1) | copy-start | bytes 786436
  23.2 2.4 %copy-start.5 = (bf16[1,1,2,256,256]{4,3,2,1,0:T(8,128)(2,1)S(1)}, bf16[1,1,2,256,256]{4,3,2,1,0:T(8,128)(2,1)}, u32[]{:S(2)}) copy-start(bf16[1,1,2,256,256]{4,3,2,1,0:T(8,128)(2,1)} %param.12) | copy-start | bytes 786436
  23.9 1.7 %collective-permute-start.6 = (bf16[2,256,256]{2,1,0:T(8,128)(2,1)S(1)}, bf16[2,256,256]{2,1,0:T(8,128)(2,1)S(1)}, u32[]{:S(2)}, u32[]{:S(2)}) collective-permute-start(bf16[2,256,256]{2,1,0:T(8,128)(2,1)S(1)} %get-tuple-element.32), channel_id=1, source_target_pairs={{0,1},{1,0},{2,3},{3,2},{4,5},{5,4},{6,7},{7,6},{8,9},{9,8},{10,11... | collective-permute-start | bytes 786440 | tf_op jit(solution)/shard_map/ppermute | solution.py:276
  29.7 1.6 %collective-permute-start.8 = (bf16[2,256,256]{2,1,0:T(8,128)(2,1)S(1)}, bf16[2,256,256]{2,1,0:T(8,128)(2,1)S(1)}, u32[]{:S(2)}, u32[]{:S(2)}) collective-permute-start(bf16[2,256,256]{2,1,0:T(8,128)(2,1)S(1)} %get-tuple-element.34), channel_id=1, source_target_pairs={{0,1},{1,0},{2,3},{3,2},{4,5},{5,4},{6,7},{7,6},{8,9},{9,8},{10,11... | collective-permute-start | bytes 786440 | tf_op jit(solution)/shard_map/ppermute | solution.py:276
  31.9 7.9 %collective-permute-start.10 = (bf16[2,128,256]{2,1,0:T(8,128)(2,1)S(1)}, bf16[2,128,256]{2,1,0:T(8,128)(2,1)S(1)}, u32[]{:S(2)}, u32[]{:S(2)}) collective-permute-start(bf16[2,128,256]{2,1,0:T(8,128)(2,1)S(1)} %get-tuple-element.39), channel_id=1, source_target_pairs={{0,4},{2,6},{4,8},{6,10},{8,12},{10,14},{12,0},{14,2},{1,5},{3,7},... | collective-permute-start | bytes 393224 | tf_op jit(solution)/shard_map/ppermute | solution.py:273
  32.0 8.4 %collective-permute-start.13 = (bf16[2,128,256]{2,1,0:T(8,128)(2,1)S(1)}, bf16[2,128,256]{2,1,0:T(8,128)(2,1)S(1)}, u32[]{:S(2)}, u32[]{:S(2)}) collective-permute-start(bf16[2,128,256]{2,1,0:T(8,128)(2,1)S(1)} %get-tuple-element.42), channel_id=1, source_target_pairs={{0,2},{2,0},{4,6},{6,4},{8,10},{10,8},{12,14},{14,12},{1,3},{3,1},... | collective-permute-start | bytes 393224 | tf_op jit(solution)/shard_map/ppermute | solution.py:273
  33.5 14.4 %collective-permute-start.9 = (bf16[2,256,256]{2,1,0:T(8,128)(2,1)S(1)}, bf16[2,256,256]{2,1,0:T(8,128)(2,1)S(1)}, u32[]{:S(2)}, u32[]{:S(2)}) collective-permute-start(bf16[2,256,256]{2,1,0:T(8,128)(2,1)S(1)} %get-tuple-element.37), channel_id=1, source_target_pairs={{0,2},{2,0},{4,6},{6,4},{8,10},{10,8},{12,14},{14,12},{1,3},{3,1},... | collective-permute-start | bytes 786440 | tf_op jit(solution)/shard_map/ppermute | solution.py:273
  35.1 12.9 %collective-permute-start.12 = (bf16[2,256,256]{2,1,0:T(8,128)(2,1)S(1)}, bf16[2,256,256]{2,1,0:T(8,128)(2,1)S(1)}, u32[]{:S(2)}, u32[]{:S(2)}) collective-permute-start(bf16[2,256,256]{2,1,0:T(8,128)(2,1)S(1)} %get-tuple-element.40), channel_id=1, source_target_pairs={{0,4},{2,6},{4,8},{6,10},{8,12},{10,14},{12,0},{14,2},{1,5},{3,7},... | collective-permute-start | bytes 786440 | tf_op jit(solution)/shard_map/ppermute | solution.py:273
  39.8 6.4 %collective-permute-start.11 = (bf16[2,128,256]{2,1,0:T(8,128)(2,1)S(1)}, bf16[2,128,256]{2,1,0:T(8,128)(2,1)S(1)}, u32[]{:S(2)}, u32[]{:S(2)}) collective-permute-start(bf16[2,128,256]{2,1,0:T(8,128)(2,1)S(1)} %shard_map.81), channel_id=1, source_target_pairs={{0,2},{2,0},{4,6},{6,4},{8,10},{10,8},{12,14},{14,12},{1,3},{3,1},... | collective-permute-start | bytes 393224 | tf_op jit(solution)/shard_map/ppermute | solution.py:273
  40.4 7.5 %collective-permute-start.14 = (bf16[2,128,256]{2,1,0:T(8,128)(2,1)S(1)}, bf16[2,128,256]{2,1,0:T(8,128)(2,1)S(1)}, u32[]{:S(2)}, u32[]{:S(2)}) collective-permute-start(bf16[2,128,256]{2,1,0:T(8,128)(2,1)S(1)} %shard_map.82), channel_id=1, source_target_pairs={{0,4},{2,6},{4,8},{6,10},{8,12},{10,14},{12,0},{14,2},{1,5},{3,7},... | collective-permute-start | bytes 393224 | tf_op jit(solution)/shard_map/ppermute | solution.py:273
